TPU v7x, 128 devices: a whole 4x4x4 slice. The times are simulated.
128 devices in a mesh: dp: 16 (over y, z_hi, core), mp: 8 (over z_lo, x).
Axes of the slice: x: 4, y: 4, z: 4 (z_hi: 2, z_lo: 2; z = z_hi * 2 + z_lo), core: 2. Of those that a mesh axis runs over, the one named last changes fastest.
Arguments:
- attn_out: bfloat16 [16384, 8192], P('dp', 'mp'), may hold values from -6 to 6
- out_weight: bfloat16 [8192, 8192], P('dp'), may hold values from -0.09375 to 0.09375
- residual: bfloat16 [16, 1024, 8192], P(None, 'mp', 'dp'), may hold values from -6 to 6
Outputs:
- layer_out: bfloat16 [16, 1024, 8192], P(None, 'mp', 'dp')
All inputs are finite; a program needn't handle non-finite values.
Results may differ from a plain program's by a relative error of at most 0.001.
Values may be sent and summed in bfloat16 or wider, within the bound.
No kernel may reach another device: no remote copies, remote signals or barrier semaphores. Data moves between devices by JAX's collectives and lax.ppermute only.
A program may use at most 192 MiB of HBM per device.

v0:
```python
import jax
import jax.numpy as jnp
from jax import lax
from jax.sharding import PartitionSpec as P


def shards(attn_out, out_weight, residual):
    by_rows = lax.all_to_all(attn_out, "mp", split_axis=0, concat_axis=1, tiled=True)
    columns = lax.all_to_all(out_weight, "dp", split_axis=1, concat_axis=0, tiled=True)
    projected = jnp.dot(
        lax.all_gather(by_rows, "dp", axis=0, tiled=True),
        columns,
        preferred_element_type=jnp.float32,
    )
    layer_out = residual.astype(jnp.float32) + projected.reshape(residual.shape)
    return layer_out.astype(jnp.bfloat16)


def solution(mesh):
    return jax.shard_map(
        shards,
        mesh=mesh,
        in_specs=(P("dp", "mp"), P("dp", None), P(None, "mp", "dp")),
        out_specs=P(None, "mp", "dp"),
        check_vma=False,
    )
```

profile of v0, /device:TPU:1, one launch (start us, length us, event | category | flops | bytes accessed | tf_op | source)
XLA Modules:
  0.0 349.2 jit_solution(1881722586007718666)
XLA Ops:
  6.5 0.0 all-gather.2.cloned.1.call-start
  6.5 32.3 %all_to_all.38 = bf16[8,128,1024]{2,1,0:T(8,128)(2,1)S(1)} all-to-all(bf16[8,128,1024]{2,1,0:T(8,128)(2,1)} %bitcast.21), channel_id=1, replica_groups=mesh['dp'=16,'mp'=8] {'mp'}, dimensions={0} | all-to-all | bytes 4194304 | tf_op jit(solution)/shard_map/all_to_all | solution.py:8
  38.9 1.5 copy.7
  40.4 0.0 all-gather.2.cloned.1.call-update
  40.4 7.5 %copy.9 = bf16[64,16,8,512]{3,2,0,1:T(8,128)(2,1)} copy(bf16[64,16,8,512]{3,2,1,0:T(8,128)(2,1)} %bitcast.17) | data formatting | bytes 16777216 | tf_op jit(solution)/shard_map/all_to_all | solution.py:9
  47.9 0.0 copy-start
  47.9 135.5 %all_to_all.39 = bf16[512,16,512]{2,0,1:T(8,128)(2,1)} all-to-all(bf16[512,16,512]{2,0,1:T(8,128)(2,1)} %bitcast.16), channel_id=1, replica_groups=mesh['dp'=16,'mp'=8] {'dp'}, dimensions={1} | all-to-all | bytes 16777216 | tf_op jit(solution)/shard_map/all_to_all | solution.py:9
  183.4 134.4 %all-gather.2.cloned.1.call-done = bf16[2048,8192]{1,0:T(8,128)(2,1)} async-done(((bf16[128,8192]{1,0:T(8,128)(2,1)}), bf16[2048,8192]{1,0:T(8,128)(2,1)}) %all-gather.2.cloned.1.call-update) | async-done | bytes 33554448 | tf_op jit(solution)/shard_map/all_gather | solution.py:11
  317.8 0.0 copy-done
  317.8 24.6 %add_convert_fusion = bf16[16,128,512]{2,1,0:T(8,128)(2,1)} fusion(bf16[16,128,512]{2,1,0:T(8,128)(2,1)S(1)} %copy-done, bf16[16,128,8192]{2,1,0:T(8,128)(2,1)} %bitcast.22, bf16[8192,512,1]{1,0,2:T(8,128)(2,1)} %bitcast.18), kind=kOutput, calls=%fused_computation.1 | convolution fusion | flops 17183014912 | bytes 46137344 | tf_op jit(solution)/shard_map/dot_general | solution.py:10
Async XLA Ops:
  6.5 311.3 %all-gather.2.cloned.1.call-start = ((), (), s32[]{:S(2)}) async-start(), calls=%async_computation.2 | async-start | bytes 35651584 | tf_op jit(solution)/shard_map/all_gather | solution.py:11
  47.9 269.9 %copy-start = (bf16[16,128,512]{2,1,0:T(8,128)(2,1)S(1)}, bf16[16,128,512]{2,1,0:T(8,128)(2,1)}, u32[]{:S(2)}) copy-start(bf16[16,128,512]{2,1,0:T(8,128)(2,1)} %param.5) | copy-start | bytes 6291460
Sparse Core Ops, SparseCore 0:
  40.5 277.2 all-gather.1
where the time goes:
time: 349 us
  blocking collectives  168 us (48%)
  waiting for transfers between devices  134 us (38%)
  matrix products  24.6 us (7%)
  between operations  13.4 us (4%)
  local copies, waits for them, and re-layouts  8.98 us (3%)
    all_to_all x1, blocking collectives, shards(): lax.all_to_all(out_weight, 'dp', split_axis=1, concat_axis=0, tiled=True)  136 us
    all_gather x1, waiting for transfers between devices, shards(): lax.all_gather(by_rows, 'dp', axis=0, tiled=True)  134 us
    all_to_all x1, blocking collectives, shards(): lax.all_to_all(attn_out, 'mp', split_axis=0, concat_axis=1, tiled=True)  32.3 us
    dot_general x1, matrix products, shards(): jnp.dot(lax.all_gather(by_rows, 'dp', axis=0, tiled=True), columns, prefe...  24.6 us
    all_to_all x1, local copies, waits for them, and re-layouts, shards(): lax.all_to_all(out_weight, 'dp', split_axis=1, concat_axis=0, tiled=True)  7.48 us
  transfers between devices with their start and end apart: 1, of which 1 were waited for; matrix products, arithmetic and copies ran while one was open for 2% of the time, Pallas kernels for 0%

commit v1 on v0

v1 whole, which is shorter than its diff:
```python
import functools
import itertools

import jax
import jax.numpy as jnp
from jax import lax
from jax.experimental import pallas as pl
from jax.experimental.pallas import tpu as pltpu
from jax.sharding import Mesh
from jax.sharding import PartitionSpec as P


AXES = ("y", "zh", "c", "zl", "x")
SIZES = (4, 2, 2, 2, 4)
Z = ("zh", "zl")
BF16, F32 = jnp.bfloat16, jnp.float32


PART = (0.03, 4.6)
FULL = (0.12, 18.4)


def code(value, scale):
    floor, unit = scale
    power = (jnp.abs(value) + floor) * (1.0 / unit)
    for _ in range(4):
        power = power * power
    return jnp.where(value < 0, -power, power).astype(BF16)


def decode(coded, scale):
    floor, unit = scale
    coded = coded.astype(F32)
    value = jnp.exp(jnp.log(jnp.abs(coded)) * 0.0625) * unit - floor
    return jnp.where(coded < 0, -value, value)


def flat(coords):
    index = 0
    for coord, size in zip(coords, SIZES):
        index = index * size + coord
    return index


def moves(target):
    return [
        (flat(s), flat(target(*s)))
        for s in itertools.product(*(range(n) for n in SIZES))
    ]


def ring(shift):
    return [(i, (i + shift) % 4) for i in range(4)]


PARTNER = [(0, 1), (1, 0), (2, 3), (3, 2)]
OTHER = [(1, 2), (2, 1), (3, 0), (0, 3)]
CORES = [(0, 1), (1, 0)]
LARGE = pltpu.CompilerParams(vmem_limit_bytes=14 << 20)
SMALL = pltpu.CompilerParams(vmem_limit_bytes=6 << 20)
VMEM = pl.BlockSpec(memory_space=pltpu.VMEM)
PREFETCH = pltpu.PrefetchScalarGridSpec


def estimate(flops, moved):
    return pl.CostEstimate(flops=flops, bytes_accessed=moved, transcendentals=0)


def columns(start, size):
    return pl.ds(pl.multiple_of(start, size), size)


def join_body(first, second, out):
    out[0] = first[...]
    out[1] = second[...]


def join(first, second):
    return pl.pallas_call(
        join_body,
        in_specs=[VMEM] * 2,
        out_specs=VMEM,
        out_shape=jax.ShapeDtypeStruct((2, *first.shape), BF16),
        compiler_params=SMALL,
        cost_estimate=estimate(1 << 28, 1 << 20),
        name="join",
    )(first, second)


def tile_body(shifts, scalars, *refs):
    halves, pieces, (own, keep, plus, minus, rows) = refs[:4], refs[4:-5], refs[-5:]
    step = pl.program_id(0)
    x, core = scalars[0], scalars[1]

    @pl.when(step == 0)
    def _():
        for s, h, k, twin in itertools.product(range(4), range(2), range(2), range(2)):
            block = halves[2 * k + h][
                lax.rem(x + s, 4), :, columns((core ^ twin) * 512, 512)
            ]
            row, col = (s * 2 + h) * 128, (k * 2 + twin) * 512
            rows[row : row + 128, col : col + 512] = block

    column, odd = columns(lax.rem(step, 2) * 256, 256), lax.rem(step, 2) == 1
    out = columns(step * 256, 256)
    for g, shift in enumerate(shifts):

        @pl.when(step >> 1 == g)
        def _():
            base = scalars[2 + shift]
            got, twin = pieces[2 * g], pieces[2 * g + 1]
            total = jnp.dot(
                rows[...],
                jnp.concatenate(
                    [
                        got[base, :, column],
                        twin[base, :, column],
                        got[1 - base, :, column],
                        twin[1 - base, :, column],
                    ],
                    axis=0,
                ),
                preferred_element_type=F32,
            )
            mine, right, across, left = (
                total[256 * s : 256 * s + 256].reshape(2, 128, 256) for s in range(4)
            )
            own[:, :, out] = mine
            keep[:, :, out] = jnp.where(odd, left, right)
            plus[:, :, out] = code(jnp.where(odd, right, across), PART)
            minus[:, :, out] = code(jnp.where(odd, across, left), PART)


def tile(scalars, rows, pieces, shifts):
    n = len(shifts)
    shape = (2, 128, 512 * n)
    return pl.pallas_call(
        functools.partial(tile_body, shifts),
        grid_spec=PREFETCH(
            num_scalar_prefetch=1,
            grid=(2 * n,),
            in_specs=[VMEM] * (4 + 2 * n),
            out_specs=[VMEM] * 4,
            scratch_shapes=[pltpu.VMEM((1024, 2048), BF16)],
        ),
        out_shape=[jax.ShapeDtypeStruct(shape, d) for d in (F32, F32, BF16, BF16)],
        compiler_params=LARGE,
        cost_estimate=estimate(n << 31, 1 << 20),
    )(
        scalars,
        *(part.reshape(4, 128, 1024) for part in rows),
        *(part for s in shifts for part in pieces[s]),
    )


def relay_body(keep, plus, minus, on, back):
    g = pl.program_id(0)
    even, odd, half = (
        columns(g * 512, 256), columns(g * 512 + 256, 256), columns(g * 256, 256),
    )
    on[:, :, half] = code(keep[:, :, even] + decode(plus[:, :, even], PART), PART)
    back[:, :, half] = code(keep[:, :, odd] + decode(minus[:, :, odd], PART), PART)


def relay(keep, plus, minus):
    shape = (2, 128, keep.shape[2] // 2)
    return pl.pallas_call(
        relay_body,
        grid=(shape[2] // 256,),
        in_specs=[VMEM] * 3,
        out_specs=[VMEM] * 2,
        out_shape=[jax.ShapeDtypeStruct(shape, BF16)] * 2,
        compiler_params=SMALL,
        cost_estimate=estimate(1 << 30, 1 << 20),
    )(keep, plus, minus)


def reduced(rows, g, own, plus, minus, on, back):
    even, odd, half = (
        columns(g * 512, 256), columns(g * 512 + 256, 256), columns(g * 256, 256),
    )
    first = decode(minus[rows, :, even], PART) + decode(on[rows, :, half], PART)
    second = decode(plus[rows, :, odd], PART) + decode(back[rows, :, half], PART)
    return (
        code(own[rows, :, even] + first, FULL),
        code(own[rows, :, odd] + second, FULL),
    )


def collect_body(*refs):
    g = pl.program_id(0)
    first, second = reduced(slice(None), g, *refs[:5])
    refs[5][:, :, columns(g * 512, 256)] = first
    refs[5][:, :, columns(g * 512 + 256, 256)] = second


def collect(*operands):
    shape = operands[0].shape
    return pl.pallas_call(
        collect_body,
        grid=(shape[2] // 512,),
        in_specs=[VMEM] * 5,
        out_specs=VMEM,
        out_shape=jax.ShapeDtypeStruct(shape, BF16),
        compiler_params=SMALL,
        cost_estimate=estimate(1 << 30, 1 << 20),
    )(*operands)


def release_body(places, scalars, *refs):
    n = len(places)
    firsts, outs = refs[5 : 5 + n], refs[5 + n :]
    j = pl.program_id(0)
    half = scalars[1] ^ j
    for g, at in enumerate(places):
        sums = reduced(half, g, *refs[:5])
        for k in range(2):

            @pl.when(j == k)
            def _():
                out = outs[2 * g + k]
                out[0] = firsts[g][half, :, at * 512 : at * 512 + 512]
                out[1, :, :256] = sums[0]
                out[1, :, 256:] = sums[1]


def release(scalars, operands, firsts):
    n = len(firsts)
    return pl.pallas_call(
        functools.partial(release_body, tuple(at for _, at in firsts)),
        grid_spec=PREFETCH(
            num_scalar_prefetch=1,
            grid=(2,),
            in_specs=[VMEM] * (5 + n),
            out_specs=[VMEM] * (2 * n),
        ),
        out_shape=[jax.ShapeDtypeStruct((2, 128, 512), BF16)] * (2 * n),
        compiler_params=SMALL,
        cost_estimate=estimate(1 << 30, 1 << 20),
    )(scalars, *operands, *(array for array, _ in firsts))


def finish_body(n, scalars, *refs):
    gots, residual, out = refs[:n], refs[n], refs[-1]
    step = pl.program_id(0)
    for q, got in enumerate(gots):

        @pl.when(step >> 1 == q)
        def _():
            total = residual[0].astype(F32) + decode(got[step & 1], FULL)
            out[0] = total.astype(BF16)


def finish(scalars, gots, residual, partial, shifts):
    n = len(gots)

    def place(t, s):
        shift = shifts[0] if len(shifts) == 1 else jnp.where(t < 4, *shifts)
        return (s[6 + shift * 4 + lax.rem(t, 4)], 0, 0)

    block = pl.BlockSpec((1, 128, 512), place)
    extra = [] if partial is None else [partial]
    return pl.pallas_call(
        functools.partial(finish_body, n),
        grid_spec=PREFETCH(
            num_scalar_prefetch=1,
            grid=(2 * n,),
            in_specs=[VMEM] * n
            + [block]
            + [pl.BlockSpec(memory_space=pl.ANY)] * len(extra),
            out_specs=block,
        ),
        out_shape=jax.ShapeDtypeStruct(residual.shape, residual.dtype),
        input_output_aliases={n + 2: 0} if extra else {},
        compiler_params=SMALL,
        cost_estimate=estimate(1 << 30, 1 << 22),
    )(scalars, *gots, residual, *extra)


def layer(attn, weight, residual):
    y, zh, c, zl, x = (lax.axis_index(a) for a in AXES)

    numbers = [x, c] + [(((y - s) % 4) >> 1) ^ zl for s in range(4)]
    for s, j, other in itertools.product(range(4), range(2), range(2)):
        numbers.append(((y + s) % 4) * 4 + (zh ^ other) * 2 + (zl ^ j))
    scalars = jnp.stack(numbers)

    piece = []
    for p in range(2):
        target = ((y >> 1) ^ p) * 8 + (x & 1) * 4 + (x >> 1) * 2 + (zl ^ zh ^ (x >> 1))
        sent = lax.dynamic_slice(weight, (0, target * 512), (512, 512))
        to = moves(
            lambda y, zh, c, zl, x: (
                ((y >> 1) ^ p) * 2 + (x & 1), x >> 1, c, zl ^ zh ^ (x >> 1),
                (y & 1) * 2 + zh,
            )
        )
        piece.append(lax.ppermute(sent, AXES, to))

    own_0 = [attn[:512], attn[512:]]
    own_1, oth_1 = [None] * 2, [None] * 2
    own_1[1] = lax.ppermute(own_0[1], Z, PARTNER)
    oth_1[0] = lax.ppermute(own_0[0], Z, OTHER)
    own_1[0] = lax.ppermute(own_0[0], Z, PARTNER)
    oth_1[1] = lax.ppermute(own_0[1], Z, OTHER)
    low = lax.ppermute(oth_1[0], Z, PARTNER)
    high = lax.ppermute(own_1[1], Z, OTHER)

    piece = join(*piece)
    pieces = {}
    for shift in (0, 1, 3, 2):
        got = lax.ppermute(piece, "y", ring(shift)) if shift else piece
        pieces[shift] = got, lax.ppermute(got, "c", CORES)

    def partials(rows, shifts):
        own, keep, plus, minus = tile(scalars, rows, pieces, shifts)
        plus = lax.ppermute(plus, "x", ring(1))
        minus = lax.ppermute(minus, "x", ring(3))
        on, back = relay(keep, plus, minus)
        on = lax.ppermute(on, "x", ring(1))
        back = lax.ppermute(back, "x", ring(3))
        return own, plus, minus, on, back

    first = {}
    for shifts in ((0,), (1, 3), (2,)):
        operands = partials(own_0 + own_1, shifts)
        coded = collect(*operands)
        for q, s in enumerate(shifts):
            first[s] = (coded, q)

    out = None
    for shifts in ((1, 3), (0,), (2,)):
        operands = partials([low, high] + oth_1, shifts)
        ready = release(scalars, operands, [first[s] for s in shifts])
        arrived = []
        for (s, j), v in zip(itertools.product(shifts, range(2)), ready):
            to = moves(lambda y, zh, c, zl, x: ((y - s) % 4, zh, zl, c ^ j, x))
            arrived.append(lax.ppermute(v, AXES, to))
        out = finish(scalars, arrived, residual, out, shifts)
    return out


def solution(mesh):
    torus = Mesh(mesh.devices.reshape(SIZES), AXES)
    return jax.shard_map(
        layer,
        mesh=torus,
        in_specs=(
            P(("y", "zh", "c"), ("zl", "x")),
            P(("y", "zh", "c"), None),
            P(None, ("zl", "x"), ("y", "zh", "c")),
        ),
        out_specs=P(None, ("zl", "x"), ("y", "zh", "c")),
        check_vma=False,
    )
```

time: 349 us -> 248 us (0.71)
  blocking collectives: 168 us -> 0 us
  starting transfers between devices: 0.01 us -> 83.7 us
  Pallas kernels: 0 us -> 58.8 us
  waiting for transfers between devices: 134 us -> 95.4 us
  matrix products: 24.6 us -> 0 us
  between operations: 13.4 us -> 0.44 us
    all_to_all x2 -> x0, blocking collectives: 168 us -> none  [the longest x1 136 us: shards(): lax.all_to_all(out_weight, 'dp', split_axis=1, concat_axis=0, tiled=True)]
    all_gather x1 -> x0, waiting for transfers between devices: 134 us -> none  [shards(): lax.all_gather(by_rows, 'dp', axis=0, tiled=True)]
    ppermute x0 -> x47, waiting for transfers between devices: none -> 95.4 us  [the longest x2 39.3 us: layer(): piece.append(lax.ppermute(sent, AXES, to))]
    ppermute x0 -> x47, starting transfers between devices: none -> 83.7 us  [the longest x6 20.5 us: partials(): minus = lax.ppermute(minus, 'x', ring(3))]
    pallas_call x0 -> x22, Pallas kernels: none -> 58.8 us  [the longest x6 39.4 us: tile(): pl.pallas_call(functools.partial(tile_body, shifts), grid_spec=PREFETCH(n...]
    dot_general x1 -> x0, matrix products: 24.6 us -> none  [shards(): jnp.dot(lax.all_gather(by_rows, 'dp', axis=0, tiled=True), columns, prefe...]
    all_to_all x2 -> x0, local copies, waits for them, and re-layouts: 8.97 us -> none  [the longest x1 7.48 us: shards(): lax.all_to_all(out_weight, 'dp', split_axis=1, concat_axis=0, tiled=True)]
    unnamed x2 -> x16, local copies, waits for them, and re-layouts: 0.01 us -> 3.83 us
  transfers between devices with their start and end apart: 1 -> 47, of which waited for: 1 -> 13; matrix products, arithmetic and copies ran while one was open for 2% -> 1% of each run, Pallas kernels for 0% -> 23%
where the time goes in v1:
time: 248 us; the launch traced here: 245 us
  waiting for transfers between devices  95.4 us (38%)
  starting transfers between devices  83.7 us (34%)
  Pallas kernels  58.8 us (24%)
  local copies, waits for them, and re-layouts  6.92 us (3%)
    pallas_call x6, Pallas kernels, tile(): pl.pallas_call(functools.partial(tile_body, shifts), grid_spec=PREFETCH(n...  39.4 us
    ppermute x2, waiting for transfers between devices, layer(): piece.append(lax.ppermute(sent, AXES, to))  39.3 us
    ppermute x3, waiting for transfers between devices, layer(): got = lax.ppermute(piece, 'y', ring(shift)) if shift else piece  29.8 us
    ppermute x6, starting transfers between devices, partials(): minus = lax.ppermute(minus, 'x', ring(3))  20.5 us
    ppermute x8, starting transfers between devices, layer(): arrived.append(lax.ppermute(v, AXES, to))  14.7 us
    ppermute x6, starting transfers between devices, partials(): back = lax.ppermute(back, 'x', ring(3))  13.3 us
    ppermute x1, waiting for transfers between devices, layer(): oth_1[1] = lax.ppermute(own_0[1], Z, OTHER)  10.2 us
    pallas_call x3, Pallas kernels, finish(): pl.pallas_call(functools.partial(finish_body, n), grid_spec=PREFETCH(num_...  8.57 us
  transfers between devices with their start and end apart: 47, of which 13 were waited for; matrix products, arithmetic and copies ran while one was open for 1% of the time, Pallas kernels for 23%

profile of v1, /device:TPU:1, one launch (start us, length us, event | category | flops | bytes accessed | tf_op | source)
XLA Modules:
  0.0 245.2 jit_solution(2439211013396447250)
XLA Ops:
  1.7 4.7 %collective-permute-start = (bf16[512,1024]{1,0:T(8,128)(2,1)S(1)}, bf16[512,1024]{1,0:T(8,128)(2,1)}, u32[]{:S(2)}, u32[]{:S(2)}) collective-permute-start(bf16[512,1024]{1,0:T(8,128)(2,1)S(1)} %get-tuple-element.96), channel_id=1, source_target_pairs={{4,16},{16,4},{20,0},{0,20},{5,17},{17,5},{21,1},{1,21},{6,18},{18... | collective-permute-start | bytes 3145736 | tf_op jit(solution)/shard_map/ppermute | solution.py:303
  8.4 3.0 %collective-permute-start.6 = (bf16[512,512]{1,0:T(8,128)(2,1)S(1)}, bf16[512,512]{1,0:T(8,128)(2,1)S(1)}, u32[]{:S(2)}, u32[]{:S(2)}) collective-permute-start(bf16[512,512]{1,0:T(8,128)(2,1)S(1)} %get-tuple-element.93), channel_id=1, source_target_pairs={{0,64},{1,96},{2,84},{3,116},{4,68},{5,100},{6,80},{7,112},{8,72},... | collective-permute-start | bytes 1572872 | tf_op jit(solution)/shard_map/ppermute | solution.py:298
  11.3 5.5 %collective-permute-start.4 = (bf16[512,1024]{1,0:T(8,128)(2,1)S(1)}, bf16[512,1024]{1,0:T(8,128)(2,1)S(1)}, u32[]{:S(2)}, u32[]{:S(2)}) collective-permute-start(bf16[512,1024]{1,0:T(8,128)(2,1)S(1)} %get-tuple-element.95), channel_id=1, source_target_pairs={{4,16},{16,4},{20,0},{0,20},{5,17},{17,5},{21,1},{1,21},{6,18},{18... | collective-permute-start | bytes 3145736 | tf_op jit(solution)/shard_map/ppermute | solution.py:305
  17.1 39.3 %collective-permute-done.6.second = bf16[512,512]{1,0:T(8,128)(2,1)S(1)} collective-permute-done((bf16[512,512]{1,0:T(8,128)(2,1)S(1)}, bf16[512,512]{1,0:T(8,128)(2,1)S(1)}, u32[]{:S(2)}, u32[]{:S(2)}) %collective-permute-start.6) | collective-permute-done | bytes 524320 | tf_op jit(solution)/shard_map/ppermute | solution.py:298
  56.5 3.8 %collective-permute-start.7 = (bf16[2,512,512]{2,1,0:T(8,128)(2,1)S(1)}, bf16[2,512,512]{2,1,0:T(8,128)(2,1)S(1)}, u32[]{:S(2)}, u32[]{:S(2)}) collective-permute-start(bf16[2,512,512]{2,1,0:T(8,128)(2,1)S(1)} %join.1.refs_4_), channel_id=1, source_target_pairs={{0,64},{32,96},{64,0},{96,32},{1,65},{33,97},{65,1},{97,33},{2,66}... | collective-permute-start | bytes 3145736 | tf_op jit(solution)/shard_map/ppermute | solution.py:312
  60.3 2.7 %collective-permute-start.33 = (bf16[2,512,512]{2,1,0:T(8,128)(2,1)S(1)}, bf16[2,512,512]{2,1,0:T(8,128)(2,1)}, u32[]{:S(2)}, u32[]{:S(2)}) collective-permute-start(bf16[2,512,512]{2,1,0:T(8,128)(2,1)S(1)} %join.1.refs_4_), channel_id=1, source_target_pairs={{0,96},{32,0},{64,32},{96,64},{1,97},{33,1},{65,33},{97,65},{2,98}... | collective-permute-start | bytes 3145736 | tf_op jit(solution)/shard_map/ppermute | solution.py:312
  62.9 10.2 %collective-permute-done.4 = bf16[512,1024]{1,0:T(8,128)(2,1)S(1)} collective-permute-done((bf16[512,1024]{1,0:T(8,128)(2,1)S(1)}, bf16[512,1024]{1,0:T(8,128)(2,1)S(1)}, u32[]{:S(2)}, u32[]{:S(2)}) %collective-permute-start.4) | collective-permute-done | bytes 1048608 | tf_op jit(solution)/shard_map/ppermute | solution.py:305
  76.6 6.1 %collective-permute-done.7.refs_4_ = bf16[2,512,512]{2,1,0:T(8,128)(2,1)S(1)} collective-permute-done((bf16[2,512,512]{2,1,0:T(8,128)(2,1)S(1)}, bf16[2,512,512]{2,1,0:T(8,128)(2,1)S(1)}, u32[]{:S(2)}, u32[]{:S(2)}) %collective-permute-start.7) | collective-permute-done | bytes 1048608 | tf_op jit(solution)/shard_map/ppermute | solution.py:312
  82.7 23.7 %collective-permute-done.31.refs_4_ = bf16[2,512,512]{2,1,0:T(8,128)(2,1)} collective-permute-done((bf16[2,512,512]{2,1,0:T(8,128)(2,1)S(1)}, bf16[2,512,512]{2,1,0:T(8,128)(2,1)}, u32[]{:S(2)}, u32[]{:S(2)}) %collective-permute-start.31) | collective-permute-done | bytes 1048608 | tf_op jit(solution)/shard_map/ppermute | solution.py:312
  108.9 5.1 %shard_map.45 = (f32[2,128,512]{2,1,0:T(8,128)S(1)}, f32[2,128,512]{2,1,0:T(8,128)S(1)}, bf16[2,128,512]{2,1,0:T(8,128)(2,1)S(1)}, bf16[2,128,512]{2,1,0:T(8,128)(2,1)S(1)}) custom-call(s32[22]{0:T(128)S(1)} %stack.91.scalars, bf16[4,128,1024]{2,1,0:T(8,128)(2,1)S(1)} %bitcast.33, bf16[4,128,1024]{2,1,0:T(8,128)(2,1)S(1)} %bitcast.30, ...), custom_call_target="tpu_custom_call" | custom-call | flops 2147483648 | bytes 1048576 | tf_op jit(solution)/shard_map/pallas_call | solution.py:137
  114.0 5.3 %collective-permute-start.25 = (bf16[2,128,512]{2,1,0:T(8,128)(2,1)S(1)}, bf16[2,128,512]{2,1,0:T(8,128)(2,1)S(1)}, u32[]{:S(2)}, u32[]{:S(2)}) collective-permute-start(bf16[2,128,512]{2,1,0:T(8,128)(2,1)S(1)} %get-tuple-element.70), channel_id=1, source_target_pairs={{0,1},{1,2},{2,3},{3,0},{4,5},{5,6},{6,7},{7,4},{8,9},{9,10},{10,1... | collective-permute-start | bytes 786440 | tf_op jit(solution)/shard_map/ppermute | solution.py:317
  119.3 10.3 %collective-permute-start.26 = (bf16[2,128,512]{2,1,0:T(8,128)(2,1)S(1)}, bf16[2,128,512]{2,1,0:T(8,128)(2,1)S(1)}, u32[]{:S(2)}, u32[]{:S(2)}) collective-permute-start(bf16[2,128,512]{2,1,0:T(8,128)(2,1)S(1)} %get-tuple-element.71), channel_id=1, source_target_pairs={{0,3},{1,0},{2,1},{3,2},{4,7},{5,4},{6,5},{7,6},{8,11},{9,8},{10,9... | collective-permute-start | bytes 786440 | tf_op jit(solution)/shard_map/ppermute | solution.py:318
  129.7 5.8 %shard_map.43 = (f32[2,128,512]{2,1,0:T(8,128)S(1)}, f32[2,128,512]{2,1,0:T(8,128)S(1)}, bf16[2,128,512]{2,1,0:T(8,128)(2,1)S(1)}, bf16[2,128,512]{2,1,0:T(8,128)(2,1)S(1)}) custom-call(s32[22]{0:T(128)S(1)} %stack.91.scalars, bf16[4,128,1024]{2,1,0:T(8,128)(2,1)} %bitcast.22.refs_0_, bf16[4,128,1024]{2,1,0:T(8,128)(2,1)} %bitcast.23.refs_1_, ...), custom_call_target="tpu_custom_call" | custom-call | flops 2147483648 | bytes 1048576 | tf_op jit(solution)/shard_map/pallas_call | solution.py:137
  135.5 2.7 %collective-permute-start.22 = (bf16[2,128,512]{2,1,0:T(8,128)(2,1)S(1)}, bf16[2,128,512]{2,1,0:T(8,128)(2,1)S(1)}, u32[]{:S(2)}, u32[]{:S(2)}) collective-permute-start(bf16[2,128,512]{2,1,0:T(8,128)(2,1)S(1)} %get-tuple-element.65), channel_id=1, source_target_pairs={{0,3},{1,0},{2,1},{3,2},{4,7},{5,4},{6,5},{7,6},{8,11},{9,8},{10,9... | collective-permute-start | bytes 786440 | tf_op jit(solution)/shard_map/ppermute | solution.py:318
  138.2 8.9 %shard_map.51 = (f32[2,128,1024]{2,1,0:T(8,128)S(1)}, f32[2,128,1024]{2,1,0:T(8,128)S(1)}, bf16[2,128,1024]{2,1,0:T(8,128)(2,1)S(1)}, bf16[2,128,1024]{2,1,0:T(8,128)(2,1)S(1)}) custom-call(s32[22]{0:T(128)S(1)} %stack.91.scalars, bf16[4,128,1024]{2,1,0:T(8,128)(2,1)S(1)} %bitcast.34, bf16[4,128,1024]{2,1,0:T(8,128)(2,1)S(1)} %bitcast.31, ...), custom_call_target="tpu_custom_call" | custom-call | flops 4294967296 | bytes 1048576 | tf_op jit(solution)/shard_map/pallas_call | solution.py:137
  147.3 9.5 %shard_map.49 = (f32[2,128,1024]{2,1,0:T(8,128)S(1)}, f32[2,128,1024]{2,1,0:T(8,128)S(1)}, bf16[2,128,1024]{2,1,0:T(8,128)(2,1)S(1)}, bf16[2,128,1024]{2,1,0:T(8,128)(2,1)S(1)}) custom-call(s32[22]{0:T(128)S(1)} %stack.91.scalars, bf16[4,128,1024]{2,1,0:T(8,128)(2,1)} %bitcast.22.refs_0_, bf16[4,128,1024]{2,1,0:T(8,128)(2,1)} %bitcast.23.refs_1_, ...), custom_call_target="tpu_custom_call" | custom-call | flops 4294967296 | bytes 1048576 | tf_op jit(solution)/shard_map/pallas_call | solution.py:137
  156.9 2.7 %collective-permute-start.36 = (bf16[2,128,1024]{2,1,0:T(8,128)(2,1)S(1)}, bf16[2,128,1024]{2,1,0:T(8,128)(2,1)S(1)}, u32[]{:S(2)}, u32[]{:S(2)}) collective-permute-start(bf16[2,128,1024]{2,1,0:T(8,128)(2,1)S(1)} %get-tuple-element.79), channel_id=1, source_target_pairs={{0,3},{1,0},{2,1},{3,2},{4,7},{5,4},{6,5},{7,6},{8,11},{9,8},{10,9... | collective-permute-start | bytes 1572872 | tf_op jit(solution)/shard_map/ppermute | solution.py:318
  161.0 5.4 %shard_map.37 = (f32[2,128,512]{2,1,0:T(8,128)S(1)}, f32[2,128,512]{2,1,0:T(8,128)S(1)}, bf16[2,128,512]{2,1,0:T(8,128)(2,1)S(1)}, bf16[2,128,512]{2,1,0:T(8,128)(2,1)S(1)}) custom-call(s32[22]{0:T(128)S(1)} %stack.91.scalars, bf16[4,128,1024]{2,1,0:T(8,128)(2,1)} %bitcast.22.refs_0_, bf16[4,128,1024]{2,1,0:T(8,128)(2,1)} %bitcast.23.refs_1_, ...), custom_call_target="tpu_custom_call" | custom-call | flops 2147483648 | bytes 1048576 | tf_op jit(solution)/shard_map/pallas_call | solution.py:137
  167.7 4.8 %shard_map.39 = (f32[2,128,512]{2,1,0:T(8,128)S(1)}, f32[2,128,512]{2,1,0:T(8,128)S(1)}, bf16[2,128,512]{2,1,0:T(8,128)(2,1)S(1)}, bf16[2,128,512]{2,1,0:T(8,128)(2,1)S(1)}) custom-call(s32[22]{0:T(128)S(1)} %stack.91.scalars, bf16[4,128,1024]{2,1,0:T(8,128)(2,1)S(1)} %bitcast.35, bf16[4,128,1024]{2,1,0:T(8,128)(2,1)S(1)} %bitcast.32, ...), custom_call_target="tpu_custom_call" | custom-call | flops 2147483648 | bytes 1048576 | tf_op jit(solution)/shard_map/pallas_call | solution.py:137
  172.5 5.4 %collective-permute-done.9.plus.refs_1_ = bf16[2,128,512]{2,1,0:T(8,128)(2,1)S(1)} collective-permute-done((bf16[2,128,512]{2,1,0:T(8,128)(2,1)S(1)}, bf16[2,128,512]{2,1,0:T(8,128)(2,1)S(1)}, u32[]{:S(2)}, u32[]{:S(2)}) %collective-permute-start.9) | collective-permute-done | bytes 262176 | tf_op jit(solution)/shard_map/ppermute | solution.py:317
  180.9 3.4 %collective-permute-start.15 = (bf16[2,128,512]{2,1,0:T(8,128)(2,1)S(1)}, bf16[2,128,512]{2,1,0:T(8,128)(2,1)S(1)}, u32[]{:S(2)}, u32[]{:S(2)}) collective-permute-start(bf16[2,128,512]{2,1,0:T(8,128)(2,1)S(1)} %get-tuple-element.57), channel_id=1, source_target_pairs={{0,3},{1,0},{2,1},{3,2},{4,7},{5,4},{6,5},{7,6},{8,11},{9,8},{10,9... | collective-permute-start | bytes 786440 | tf_op jit(solution)/shard_map/ppermute | solution.py:318
  185.3 2.7 %collective-permute-start.42 = (bf16[2,128,512]{2,1,0:T(8,128)(2,1)S(1)}, bf16[2,128,512]{2,1,0:T(8,128)(2,1)S(1)}, u32[]{:S(2)}, u32[]{:S(2)}) collective-permute-start(bf16[2,128,512]{2,1,0:T(8,128)(2,1)S(1)} %get-tuple-element.88), channel_id=1, source_target_pairs={{0,3},{1,0},{2,1},{3,2},{4,7},{5,4},{6,5},{7,6},{8,11},{9,8},{10,9... | collective-permute-start | bytes 786440 | tf_op jit(solution)/shard_map/ppermute | solution.py:321
  188.9 2.7 %collective-permute-start.38 = (bf16[2,128,512]{2,1,0:T(8,128)(2,1)S(1)}, bf16[2,128,512]{2,1,0:T(8,128)(2,1)S(1)}, u32[]{:S(2)}, u32[]{:S(2)}) collective-permute-start(bf16[2,128,512]{2,1,0:T(8,128)(2,1)S(1)} %get-tuple-element.82), channel_id=1, source_target_pairs={{0,3},{1,0},{2,1},{3,2},{4,7},{5,4},{6,5},{7,6},{8,11},{9,8},{10,9... | collective-permute-start | bytes 786440 | tf_op jit(solution)/shard_map/ppermute | solution.py:321
  207.1 2.6 %collective-permute-start.17 = (bf16[2,128,256]{2,1,0:T(8,128)(2,1)S(1)}, bf16[2,128,256]{2,1,0:T(8,128)(2,1)S(1)}, u32[]{:S(2)}, u32[]{:S(2)}) collective-permute-start(bf16[2,128,256]{2,1,0:T(8,128)(2,1)S(1)} %get-tuple-element.60), channel_id=1, source_target_pairs={{0,3},{1,0},{2,1},{3,2},{4,7},{5,4},{6,5},{7,6},{8,11},{9,8},{10,9... | collective-permute-start | bytes 393224 | tf_op jit(solution)/shard_map/ppermute | solution.py:321
  209.6 4.0 %collective-permute-start.43 = (bf16[2,128,512]{2,1,0:T(8,128)(2,1)S(1)}, bf16[2,128,512]{2,1,0:T(8,128)(2,1)S(1)}, u32[]{:S(2)}, u32[]{:S(2)}) collective-permute-start(bf16[2,128,512]{2,1,0:T(8,128)(2,1)S(1)} %get-tuple-element.89), channel_id=1, source_target_pairs={{0,96},{1,97},{2,98},{3,99},{4,104},{5,105},{6,106},{7,107},{8,100... | collective-permute-start | bytes 786440 | tf_op jit(solution)/shard_map/ppermute | solution.py:338
  219.7 4.2 %collective-permute-start.29 = (bf16[2,128,512]{2,1,0:T(8,128)(2,1)S(1)}, bf16[2,128,512]{2,1,0:T(8,128)(2,1)S(1)}, u32[]{:S(2)}, u32[]{:S(2)}) collective-permute-start(bf16[2,128,512]{2,1,0:T(8,128)(2,1)S(1)} %get-tuple-element.75), channel_id=1, source_target_pairs={{0,0},{1,1},{2,2},{3,3},{4,8},{5,9},{6,10},{7,11},{8,4},{9,5},{10,... | collective-permute-start | bytes 786440 | tf_op jit(solution)/shard_map/ppermute | solution.py:338
  225.3 3.8 %collective-permute-start.18 = (bf16[2,128,512]{2,1,0:T(8,128)(2,1)S(1)}, bf16[2,128,512]{2,1,0:T(8,128)(2,1)S(1)}, u32[]{:S(2)}, u32[]{:S(2)}) collective-permute-start(bf16[2,128,512]{2,1,0:T(8,128)(2,1)S(1)} %get-tuple-element.61), channel_id=1, source_target_pairs={{0,64},{1,65},{2,66},{3,67},{4,72},{5,73},{6,74},{7,75},{8,68},{9,... | collective-permute-start | bytes 786440 | tf_op jit(solution)/shard_map/ppermute | solution.py:338
  230.3 3.9 %shard_map.55.refs_3_ = bf16[16,128,512]{2,1,0:T(8,128)(2,1)} custom-call(s32[22]{0:T(128)S(1)} %stack.91.scalars, bf16[2,128,512]{2,1,0:T(8,128)(2,1)S(1)} %collective-permute-done.43.refs_0_, bf16[2,128,512]{2,1,0:T(8,128)(2,1)S(1)} %collective-permute-done.44.refs_1_, bf16[2,128,512]{2,1,0:T(8,128)(2,1)S(1)} %collective-permute-done.45.refs_2_, ...), custom_call_target="tpu_custom_call" | custom-call | flops 1073741824 | bytes 4194304 | tf_op jit(solution)/shard_map/pallas_call | solution.py:263
  234.2 2.6 %collective-permute-done.29.refs_0_ = bf16[2,128,512]{2,1,0:T(8,128)(2,1)S(1)} collective-permute-done((bf16[2,128,512]{2,1,0:T(8,128)(2,1)S(1)}, bf16[2,128,512]{2,1,0:T(8,128)(2,1)S(1)}, u32[]{:S(2)}, u32[]{:S(2)}) %collective-permute-start.29) | collective-permute-done | bytes 262176 | tf_op jit(solution)/shard_map/ppermute | solution.py:338
  237.1 2.3 shard_map.56.refs_3_
  239.4 3.5 %collective-permute-done.19.refs_1_ = bf16[2,128,512]{2,1,0:T(8,128)(2,1)S(1)} collective-permute-done((bf16[2,128,512]{2,1,0:T(8,128)(2,1)S(1)}, bf16[2,128,512]{2,1,0:T(8,128)(2,1)S(1)}, u32[]{:S(2)}, u32[]{:S(2)}) %collective-permute-start.19) | collective-permute-done | bytes 262176 | tf_op jit(solution)/shard_map/ppermute | solution.py:338
  242.8 2.3 shard_map.57
  (103 shorter events, 42.0 us)
Async XLA Ops:
  1.7 58.5 %collective-permute-start = (bf16[512,1024]{1,0:T(8,128)(2,1)S(1)}, bf16[512,1024]{1,0:T(8,128)(2,1)}, u32[]{:S(2)}, u32[]{:S(2)}) collective-permute-start(bf16[512,1024]{1,0:T(8,128)(2,1)S(1)} %get-tuple-element.96), channel_id=1, source_target_pairs={{4,16},{16,4},{20,0},{0,20},{5,17},{17,5},{21,1},{1,21},{6,18},{18... | collective-permute-start | bytes 3145736 | tf_op jit(solution)/shard_map/ppermute | solution.py:303
  6.4 53.9 %collective-permute-start.2 = (bf16[512,1024]{1,0:T(8,128)(2,1)S(1)}, bf16[512,1024]{1,0:T(8,128)(2,1)}, u32[]{:S(2)}, u32[]{:S(2)}) collective-permute-start(bf16[512,1024]{1,0:T(8,128)(2,1)S(1)} %get-tuple-element.95), channel_id=1, source_target_pairs={{0,4},{4,0},{16,20},{20,16},{1,5},{5,1},{17,21},{21,17},{2,6},{6,2... | collective-permute-start | bytes 3145736 | tf_op jit(solution)/shard_map/ppermute | solution.py:302
  8.4 48.0 %collective-permute-start.6 = (bf16[512,512]{1,0:T(8,128)(2,1)S(1)}, bf16[512,512]{1,0:T(8,128)(2,1)S(1)}, u32[]{:S(2)}, u32[]{:S(2)}) collective-permute-start(bf16[512,512]{1,0:T(8,128)(2,1)S(1)} %get-tuple-element.93), channel_id=1, source_target_pairs={{0,64},{1,96},{2,84},{3,116},{4,68},{5,100},{6,80},{7,112},{8,72},... | collective-permute-start | bytes 1572872 | tf_op jit(solution)/shard_map/ppermute | solution.py:298
  11.3 61.8 %collective-permute-start.4 = (bf16[512,1024]{1,0:T(8,128)(2,1)S(1)}, bf16[512,1024]{1,0:T(8,128)(2,1)S(1)}, u32[]{:S(2)}, u32[]{:S(2)}) collective-permute-start(bf16[512,1024]{1,0:T(8,128)(2,1)S(1)} %get-tuple-element.95), channel_id=1, source_target_pairs={{4,16},{16,4},{20,0},{0,20},{5,17},{17,5},{21,1},{1,21},{6,18},{18... | collective-permute-start | bytes 3145736 | tf_op jit(solution)/shard_map/ppermute | solution.py:305
  16.8 58.8 %collective-permute-start.13 = (bf16[512,1024]{1,0:T(8,128)(2,1)S(1)}, bf16[512,1024]{1,0:T(8,128)(2,1)S(1)}, u32[]{:S(2)}, u32[]{:S(2)}) collective-permute-start(bf16[512,1024]{1,0:T(8,128)(2,1)S(1)} %get-tuple-element.96), channel_id=1, source_target_pairs={{0,4},{4,0},{16,20},{20,16},{1,5},{5,1},{17,21},{21,17},{2,6},{6,2... | collective-permute-start | bytes 3145736 | tf_op jit(solution)/shard_map/ppermute | solution.py:304
  56.5 26.3 %collective-permute-start.7 = (bf16[2,512,512]{2,1,0:T(8,128)(2,1)S(1)}, bf16[2,512,512]{2,1,0:T(8,128)(2,1)S(1)}, u32[]{:S(2)}, u32[]{:S(2)}) collective-permute-start(bf16[2,512,512]{2,1,0:T(8,128)(2,1)S(1)} %join.1.refs_4_), channel_id=1, source_target_pairs={{0,64},{32,96},{64,0},{96,32},{1,65},{33,97},{65,1},{97,33},{2,66}... | collective-permute-start | bytes 3145736 | tf_op jit(solution)/shard_map/ppermute | solution.py:312
  60.3 46.2 %collective-permute-start.31 = (bf16[2,512,512]{2,1,0:T(8,128)(2,1)S(1)}, bf16[2,512,512]{2,1,0:T(8,128)(2,1)}, u32[]{:S(2)}, u32[]{:S(2)}) collective-permute-start(bf16[2,512,512]{2,1,0:T(8,128)(2,1)S(1)} %join.1.refs_4_), channel_id=1, source_target_pairs={{0,32},{32,64},{64,96},{96,0},{1,33},{33,65},{65,97},{97,1},{2,34}... | collective-permute-start | bytes 3145736 | tf_op jit(solution)/shard_map/ppermute | solution.py:312
  60.3 46.7 %collective-permute-start.33 = (bf16[2,512,512]{2,1,0:T(8,128)(2,1)S(1)}, bf16[2,512,512]{2,1,0:T(8,128)(2,1)}, u32[]{:S(2)}, u32[]{:S(2)}) collective-permute-start(bf16[2,512,512]{2,1,0:T(8,128)(2,1)S(1)} %join.1.refs_4_), channel_id=1, source_target_pairs={{0,96},{32,0},{64,32},{96,64},{1,97},{33,1},{65,33},{97,65},{2,98}... | collective-permute-start | bytes 3145736 | tf_op jit(solution)/shard_map/ppermute | solution.py:312
  74.1 33.0 %collective-permute-start.20 = (bf16[2,512,512]{2,1,0:T(8,128)(2,1)S(1)}, bf16[2,512,512]{2,1,0:T(8,128)(2,1)}, u32[]{:S(2)}, u32[]{:S(2)}) collective-permute-start(bf16[2,512,512]{2,1,0:T(8,128)(2,1)S(1)} %join.1.refs_4_), channel_id=1, source_target_pairs={{0,8},{8,0},{1,9},{9,1},{2,10},{10,2},{3,11},{11,3},{4,12},{12,4},... | collective-permute-start | bytes 3145736 | tf_op jit(solution)/shard_map/ppermute | solution.py:313
  76.6 37.4 %collective-permute-start.1 = (bf16[512,1024]{1,0:T(8,128)(2,1)}, bf16[512,1024]{1,0:T(8,128)(2,1)}, u32[]{:S(2)}, u32[]{:S(2)}) collective-permute-start(bf16[512,1024]{1,0:T(8,128)(2,1)} %collective-permute-done), channel_id=1, source_target_pairs={{0,4},{4,0},{16,20},{20,16},{1,5},{5,1},{17,21},{21,17},{2,6},{6,2... | collective-permute-start | bytes 3145736 | tf_op jit(solution)/shard_map/ppermute | solution.py:306
  82.7 36.6 %collective-permute-start.3 = (bf16[512,1024]{1,0:T(8,128)(2,1)}, bf16[512,1024]{1,0:T(8,128)(2,1)}, u32[]{:S(2)}, u32[]{:S(2)}) collective-permute-start(bf16[512,1024]{1,0:T(8,128)(2,1)} %collective-permute-done.2), channel_id=1, source_target_pairs={{4,16},{16,4},{20,0},{0,20},{5,17},{17,5},{21,1},{1,21},{6,18},{18... | collective-permute-start | bytes 3145736 | tf_op jit(solution)/shard_map/ppermute | solution.py:307
  106.4 29.0 %collective-permute-start.32 = (bf16[2,512,512]{2,1,0:T(8,128)(2,1)}, bf16[2,512,512]{2,1,0:T(8,128)(2,1)}, u32[]{:S(2)}, u32[]{:S(2)}) collective-permute-start(bf16[2,512,512]{2,1,0:T(8,128)(2,1)} %collective-permute-done.31.refs_4_), channel_id=1, source_target_pairs={{0,8},{8,0},{1,9},{9,1},{2,10},{10,2},{3,11},{11,3},{4,12},{12,4},... | collective-permute-start | bytes 3145736 | tf_op jit(solution)/shard_map/ppermute | solution.py:313
  106.9 28.6 %collective-permute-start.34 = (bf16[2,512,512]{2,1,0:T(8,128)(2,1)}, bf16[2,512,512]{2,1,0:T(8,128)(2,1)}, u32[]{:S(2)}, u32[]{:S(2)}) collective-permute-start(bf16[2,512,512]{2,1,0:T(8,128)(2,1)} %collective-permute-done.33.refs_6_), channel_id=1, source_target_pairs={{0,8},{8,0},{1,9},{9,1},{2,10},{10,2},{3,11},{11,3},{4,12},{12,4},... | collective-permute-start | bytes 3145736 | tf_op jit(solution)/shard_map/ppermute | solution.py:313
  107.2 52.5 %collective-permute-start.8 = (bf16[2,512,512]{2,1,0:T(8,128)(2,1)}, bf16[2,512,512]{2,1,0:T(8,128)(2,1)S(1)}, u32[]{:S(2)}, u32[]{:S(2)}) collective-permute-start(bf16[2,512,512]{2,1,0:T(8,128)(2,1)} %copy-done.4), channel_id=1, source_target_pairs={{0,8},{8,0},{1,9},{9,1},{2,10},{10,2},{3,11},{11,3},{4,12},{12,4},... | collective-permute-start | bytes 3145736 | tf_op jit(solution)/shard_map/ppermute | solution.py:313
  114.0 33.0 %collective-permute-start.25 = (bf16[2,128,512]{2,1,0:T(8,128)(2,1)S(1)}, bf16[2,128,512]{2,1,0:T(8,128)(2,1)S(1)}, u32[]{:S(2)}, u32[]{:S(2)}) collective-permute-start(bf16[2,128,512]{2,1,0:T(8,128)(2,1)S(1)} %get-tuple-element.70), channel_id=1, source_target_pairs={{0,1},{1,2},{2,3},{3,0},{4,5},{5,6},{6,7},{7,4},{8,9},{9,10},{10,1... | collective-permute-start | bytes 786440 | tf_op jit(solution)/shard_map/ppermute | solution.py:317
  119.3 37.5 %collective-permute-start.26 = (bf16[2,128,512]{2,1,0:T(8,128)(2,1)S(1)}, bf16[2,128,512]{2,1,0:T(8,128)(2,1)S(1)}, u32[]{:S(2)}, u32[]{:S(2)}) collective-permute-start(bf16[2,128,512]{2,1,0:T(8,128)(2,1)S(1)} %get-tuple-element.71), channel_id=1, source_target_pairs={{0,3},{1,0},{2,1},{3,2},{4,7},{5,4},{6,5},{7,6},{8,11},{9,8},{10,9... | collective-permute-start | bytes 786440 | tf_op jit(solution)/shard_map/ppermute | solution.py:318
  135.4 21.5 %collective-permute-start.21 = (bf16[2,128,512]{2,1,0:T(8,128)(2,1)S(1)}, bf16[2,128,512]{2,1,0:T(8,128)(2,1)S(1)}, u32[]{:S(2)}, u32[]{:S(2)}) collective-permute-start(bf16[2,128,512]{2,1,0:T(8,128)(2,1)S(1)} %get-tuple-element.64), channel_id=1, source_target_pairs={{0,1},{1,2},{2,3},{3,0},{4,5},{5,6},{6,7},{7,4},{8,9},{9,10},{10,1... | collective-permute-start | bytes 786440 | tf_op jit(solution)/shard_map/ppermute | solution.py:317
  135.5 31.0 %collective-permute-start.22 = (bf16[2,128,512]{2,1,0:T(8,128)(2,1)S(1)}, bf16[2,128,512]{2,1,0:T(8,128)(2,1)S(1)}, u32[]{:S(2)}, u32[]{:S(2)}) collective-permute-start(bf16[2,128,512]{2,1,0:T(8,128)(2,1)S(1)} %get-tuple-element.65), channel_id=1, source_target_pairs={{0,3},{1,0},{2,1},{3,2},{4,7},{5,4},{6,5},{7,6},{8,11},{9,8},{10,9... | collective-permute-start | bytes 786440 | tf_op jit(solution)/shard_map/ppermute | solution.py:318
  147.1 30.8 %collective-permute-start.39 = (bf16[2,128,1024]{2,1,0:T(8,128)(2,1)S(1)}, bf16[2,128,1024]{2,1,0:T(8,128)(2,1)S(1)}, u32[]{:S(2)}, u32[]{:S(2)}) collective-permute-start(bf16[2,128,1024]{2,1,0:T(8,128)(2,1)S(1)} %get-tuple-element.84), channel_id=1, source_target_pairs={{0,1},{1,2},{2,3},{3,0},{4,5},{5,6},{6,7},{7,4},{8,9},{9,10},{10,1... | collective-permute-start | bytes 1572872 | tf_op jit(solution)/shard_map/ppermute | solution.py:317
  156.8 28.3 %collective-permute-start.35 = (bf16[2,128,1024]{2,1,0:T(8,128)(2,1)S(1)}, bf16[2,128,1024]{2,1,0:T(8,128)(2,1)S(1)}, u32[]{:S(2)}, u32[]{:S(2)}) collective-permute-start(bf16[2,128,1024]{2,1,0:T(8,128)(2,1)S(1)} %get-tuple-element.78), channel_id=1, source_target_pairs={{0,1},{1,2},{2,3},{3,0},{4,5},{5,6},{6,7},{7,4},{8,9},{9,10},{10,1... | collective-permute-start | bytes 1572872 | tf_op jit(solution)/shard_map/ppermute | solution.py:317
  156.9 28.3 %collective-permute-start.36 = (bf16[2,128,1024]{2,1,0:T(8,128)(2,1)S(1)}, bf16[2,128,1024]{2,1,0:T(8,128)(2,1)S(1)}, u32[]{:S(2)}, u32[]{:S(2)}) collective-permute-start(bf16[2,128,1024]{2,1,0:T(8,128)(2,1)S(1)} %get-tuple-element.79), channel_id=1, source_target_pairs={{0,3},{1,0},{2,1},{3,2},{4,7},{5,4},{6,5},{7,6},{8,11},{9,8},{10,9... | collective-permute-start | bytes 1572872 | tf_op jit(solution)/shard_map/ppermute | solution.py:318
  159.7 21.3 %collective-permute-start.40 = (bf16[2,128,1024]{2,1,0:T(8,128)(2,1)S(1)}, bf16[2,128,1024]{2,1,0:T(8,128)(2,1)S(1)}, u32[]{:S(2)}, u32[]{:S(2)}) collective-permute-start(bf16[2,128,1024]{2,1,0:T(8,128)(2,1)S(1)} %get-tuple-element.85), channel_id=1, source_target_pairs={{0,3},{1,0},{2,1},{3,2},{4,7},{5,4},{6,5},{7,6},{8,11},{9,8},{10,9... | collective-permute-start | bytes 1572872 | tf_op jit(solution)/shard_map/ppermute | solution.py:318
  188.8 13.8 %collective-permute-start.37 = (bf16[2,128,512]{2,1,0:T(8,128)(2,1)S(1)}, bf16[2,128,512]{2,1,0:T(8,128)(2,1)S(1)}, u32[]{:S(2)}, u32[]{:S(2)}) collective-permute-start(bf16[2,128,512]{2,1,0:T(8,128)(2,1)S(1)} %get-tuple-element.81), channel_id=1, source_target_pairs={{0,1},{1,2},{2,3},{3,0},{4,5},{5,6},{6,7},{7,4},{8,9},{9,10},{10,1... | collective-permute-start | bytes 786440 | tf_op jit(solution)/shard_map/ppermute | solution.py:320
  188.9 14.5 %collective-permute-start.38 = (bf16[2,128,512]{2,1,0:T(8,128)(2,1)S(1)}, bf16[2,128,512]{2,1,0:T(8,128)(2,1)S(1)}, u32[]{:S(2)}, u32[]{:S(2)}) collective-permute-start(bf16[2,128,512]{2,1,0:T(8,128)(2,1)S(1)} %get-tuple-element.82), channel_id=1, source_target_pairs={{0,3},{1,0},{2,1},{3,2},{4,7},{5,4},{6,5},{7,6},{8,11},{9,8},{10,9... | collective-permute-start | bytes 786440 | tf_op jit(solution)/shard_map/ppermute | solution.py:321
  200.6 13.7 %collective-permute-start.24 = (bf16[2,128,256]{2,1,0:T(8,128)(2,1)S(1)}, bf16[2,128,256]{2,1,0:T(8,128)(2,1)S(1)}, u32[]{:S(2)}, u32[]{:S(2)}) collective-permute-start(bf16[2,128,256]{2,1,0:T(8,128)(2,1)S(1)} %get-tuple-element.68), channel_id=1, source_target_pairs={{0,3},{1,0},{2,1},{3,2},{4,7},{5,4},{6,5},{7,6},{8,11},{9,8},{10,9... | collective-permute-start | bytes 393224 | tf_op jit(solution)/shard_map/ppermute | solution.py:321
  202.6 13.2 %collective-permute-start.11 = (bf16[2,128,256]{2,1,0:T(8,128)(2,1)S(1)}, bf16[2,128,256]{2,1,0:T(8,128)(2,1)S(1)}, u32[]{:S(2)}, u32[]{:S(2)}) collective-permute-start(bf16[2,128,256]{2,1,0:T(8,128)(2,1)S(1)} %get-tuple-element.53), channel_id=1, source_target_pairs={{0,1},{1,2},{2,3},{3,0},{4,5},{5,6},{6,7},{7,4},{8,9},{9,10},{10,1... | collective-permute-start | bytes 393224 | tf_op jit(solution)/shard_map/ppermute | solution.py:320
  203.4 13.1 %collective-permute-start.16 = (bf16[2,128,256]{2,1,0:T(8,128)(2,1)S(1)}, bf16[2,128,256]{2,1,0:T(8,128)(2,1)S(1)}, u32[]{:S(2)}, u32[]{:S(2)}) collective-permute-start(bf16[2,128,256]{2,1,0:T(8,128)(2,1)S(1)} %get-tuple-element.59), channel_id=1, source_target_pairs={{0,1},{1,2},{2,3},{3,0},{4,5},{5,6},{6,7},{7,4},{8,9},{9,10},{10,1... | collective-permute-start | bytes 393224 | tf_op jit(solution)/shard_map/ppermute | solution.py:320
  209.6 14.2 %collective-permute-start.43 = (bf16[2,128,512]{2,1,0:T(8,128)(2,1)S(1)}, bf16[2,128,512]{2,1,0:T(8,128)(2,1)S(1)}, u32[]{:S(2)}, u32[]{:S(2)}) collective-permute-start(bf16[2,128,512]{2,1,0:T(8,128)(2,1)S(1)} %get-tuple-element.89), channel_id=1, source_target_pairs={{0,96},{1,97},{2,98},{3,99},{4,104},{5,105},{6,106},{7,107},{8,100... | collective-permute-start | bytes 786440 | tf_op jit(solution)/shard_map/ppermute | solution.py:338
  219.7 17.2 %collective-permute-start.29 = (bf16[2,128,512]{2,1,0:T(8,128)(2,1)S(1)}, bf16[2,128,512]{2,1,0:T(8,128)(2,1)S(1)}, u32[]{:S(2)}, u32[]{:S(2)}) collective-permute-start(bf16[2,128,512]{2,1,0:T(8,128)(2,1)S(1)} %get-tuple-element.75), channel_id=1, source_target_pairs={{0,0},{1,1},{2,2},{3,3},{4,8},{5,9},{6,10},{7,11},{8,4},{9,5},{10,... | collective-permute-start | bytes 786440 | tf_op jit(solution)/shard_map/ppermute | solution.py:338
  223.9 13.2 %collective-permute-start.30 = (bf16[2,128,512]{2,1,0:T(8,128)(2,1)S(1)}, bf16[2,128,512]{2,1,0:T(8,128)(2,1)S(1)}, u32[]{:S(2)}, u32[]{:S(2)}) collective-permute-start(bf16[2,128,512]{2,1,0:T(8,128)(2,1)S(1)} %get-tuple-element.76), channel_id=1, source_target_pairs={{0,4},{1,5},{2,6},{3,7},{4,12},{5,13},{6,14},{7,15},{8,0},{9,1},{1... | collective-permute-start | bytes 786440 | tf_op jit(solution)/shard_map/ppermute | solution.py:338
  225.3 14.1 %collective-permute-start.18 = (bf16[2,128,512]{2,1,0:T(8,128)(2,1)S(1)}, bf16[2,128,512]{2,1,0:T(8,128)(2,1)S(1)}, u32[]{:S(2)}, u32[]{:S(2)}) collective-permute-start(bf16[2,128,512]{2,1,0:T(8,128)(2,1)S(1)} %get-tuple-element.61), channel_id=1, source_target_pairs={{0,64},{1,65},{2,66},{3,67},{4,72},{5,73},{6,74},{7,75},{8,68},{9,... | collective-permute-start | bytes 786440 | tf_op jit(solution)/shard_map/ppermute | solution.py:338
  229.1 13.8 %collective-permute-start.19 = (bf16[2,128,512]{2,1,0:T(8,128)(2,1)S(1)}, bf16[2,128,512]{2,1,0:T(8,128)(2,1)S(1)}, u32[]{:S(2)}, u32[]{:S(2)}) collective-permute-start(bf16[2,128,512]{2,1,0:T(8,128)(2,1)S(1)} %get-tuple-element.62), channel_id=1, source_target_pairs={{0,68},{1,69},{2,70},{3,71},{4,76},{5,77},{6,78},{7,79},{8,64},{9,... | collective-permute-start | bytes 786440 | tf_op jit(solution)/shard_map/ppermute | solution.py:338
  (23 other events, 233.1 us)

commit v2 on v1

--- a/solution.py
+++ b/solution.py
@@ -87,8 +87,8 @@
     )(first, second)
 
 
-def tile_body(shifts, scalars, *refs):
-    halves, pieces, (own, keep, plus, minus, rows) = refs[:4], refs[4:-5], refs[-5:]
+def tile_body(shifts, relayed, scalars, *refs):
+    halves, pieces, (own, third, plus, minus, rows) = refs[:4], refs[4:-5], refs[-5:]
     step = pl.program_id(0)
     x, core = scalars[0], scalars[1]
 
@@ -126,16 +126,21 @@
                 total[256 * s : 256 * s + 256].reshape(2, 128, 256) for s in range(4)
             )
             own[:, :, out] = mine
-            keep[:, :, out] = jnp.where(odd, left, right)
-            plus[:, :, out] = code(jnp.where(odd, right, across), PART)
-            minus[:, :, out] = code(jnp.where(odd, across, left), PART)
-
-
-def tile(scalars, rows, pieces, shifts):
+            if relayed:
+                third[:, :, out] = jnp.where(odd, left, right)
+                plus[:, :, out] = code(jnp.where(odd, right, across), PART)
+                minus[:, :, out] = code(jnp.where(odd, across, left), PART)
+            else:
+                third[:, :, out] = code(across, PART)
+                plus[:, :, out] = code(right, PART)
+                minus[:, :, out] = code(left, PART)
+
+
+def tile(scalars, rows, pieces, shifts, relayed):
     n = len(shifts)
     shape = (2, 128, 512 * n)
     return pl.pallas_call(
-        functools.partial(tile_body, shifts),
+        functools.partial(tile_body, shifts, relayed),
         grid_spec=PREFETCH(
             num_scalar_prefetch=1,
             grid=(2 * n,),
@@ -143,7 +148,10 @@
             out_specs=[VMEM] * 4,
             scratch_shapes=[pltpu.VMEM((1024, 2048), BF16)],
         ),
-        out_shape=[jax.ShapeDtypeStruct(shape, d) for d in (F32, F32, BF16, BF16)],
+        out_shape=[
+            jax.ShapeDtypeStruct(shape, d)
+            for d in (F32, F32 if relayed else BF16, BF16, BF16)
+        ],
         compiler_params=LARGE,
         cost_estimate=estimate(n << 31, 1 << 20),
     )(
@@ -187,11 +195,12 @@
     )
 
 
-def collect_body(*refs):
-    g = pl.program_id(0)
-    first, second = reduced(slice(None), g, *refs[:5])
-    refs[5][:, :, columns(g * 512, 256)] = first
-    refs[5][:, :, columns(g * 512 + 256, 256)] = second
+def collect_body(own, across, plus, minus, out):
+    part = columns(pl.program_id(0) * 512, 512)
+    total = own[:, :, part]
+    for ref in (across, plus, minus):
+        total = total + decode(ref[:, :, part], PART)
+    out[:, :, part] = code(total, FULL)
 
 
 def collect(*operands):
@@ -199,7 +208,7 @@
     return pl.pallas_call(
         collect_body,
         grid=(shape[2] // 512,),
-        in_specs=[VMEM] * 5,
+        in_specs=[VMEM] * 4,
         out_specs=VMEM,
         out_shape=jax.ShapeDtypeStruct(shape, BF16),
         compiler_params=SMALL,
@@ -277,6 +286,10 @@
     )(scalars, *gots, residual, *extra)
 
 
+OWN = {"own_a": (0,), "own_b": (1, 3), "own_c": (2,)}
+OTH = {"oth_a": (1, 3), "oth_b": (2,), "oth_c": (0,)}
+
+
 def layer(attn, weight, residual):
     y, zh, c, zl, x = (lax.axis_index(a) for a in AXES)
 
@@ -312,26 +325,28 @@
         got = lax.ppermute(piece, "y", ring(shift)) if shift else piece
         pieces[shift] = got, lax.ppermute(got, "c", CORES)
 
-    def partials(rows, shifts):
-        own, keep, plus, minus = tile(scalars, rows, pieces, shifts)
+    first, out = {}, None
+    for shifts in OWN.values():
+        own, across, plus, minus = tile(scalars, own_0 + own_1, pieces, shifts, False)
+        plus = lax.ppermute(plus, "x", ring(1))
+        minus = lax.ppermute(minus, "x", ring(3))
+        across = lax.ppermute(across, "x", ring(2))
+        coded = collect(own, across, plus, minus)
+        for q, s in enumerate(shifts):
+            first[s] = (coded, q)
+    for shifts in OTH.values():
+        own, keep, plus, minus = tile(
+            scalars, [low, high] + oth_1, pieces, shifts, True
+        )
         plus = lax.ppermute(plus, "x", ring(1))
         minus = lax.ppermute(minus, "x", ring(3))
         on, back = relay(keep, plus, minus)
         on = lax.ppermute(on, "x", ring(1))
         back = lax.ppermute(back, "x", ring(3))
-        return own, plus, minus, on, back
-
-    first = {}
-    for shifts in ((0,), (1, 3), (2,)):
-        operands = partials(own_0 + own_1, shifts)
-        coded = collect(*operands)
-        for q, s in enumerate(shifts):
-            first[s] = (coded, q)
-
-    out = None
-    for shifts in ((1, 3), (0,), (2,)):
-        operands = partials([low, high] + oth_1, shifts)
-        ready = release(scalars, operands, [first[s] for s in shifts])
+        ready = release(
+            scalars, (own, plus, minus, on, back),
+            [first[s] for s in shifts],
+        )
         arrived = []
         for (s, j), v in zip(itertools.product(shifts, range(2)), ready):
             to = moves(lambda y, zh, c, zl, x: ((y - s) % 4, zh, zl, c ^ j, x))

time: 248 us -> 244 us (0.984)
  starting transfers between devices: 83.7 us -> 71.8 us
  waiting for transfers between devices: 95.4 us -> 103 us
    ppermute x24 -> x21, starting transfers between devices: 45.8 us -> 28.9 us  [the longest x6 8.92 us: layer(): minus = lax.ppermute(minus, 'x', ring(3))]
    ppermute x24 -> x21, waiting for transfers between devices: 9.35 us -> 18 us  [the longest x6 9.14 us: layer(): plus = lax.ppermute(plus, 'x', ring(1))]
    ppermute x3, waiting for transfers between devices: 29.8 us -> 23.1 us  [layer(): got = lax.ppermute(piece, 'y', ring(shift)) if shift else piece]
    ppermute x8, waiting for transfers between devices: 6.7 us -> 10.4 us  [layer(): arrived.append(lax.ppermute(v, AXES, to))]
    ppermute x1, starting transfers between devices: 0.01 us -> 3.41 us  [layer(): high = lax.ppermute(own_1[1], Z, OTHER)]
    unnamed x16 -> x18, local copies, waits for them, and re-layouts: 3.83 us -> 5.46 us
  transfers between devices with their start and end apart: 47 -> 44, of which waited for: 13 -> 13; matrix products, arithmetic and copies ran while one was open for 1% -> 1% of each run, Pallas kernels for 23% -> 23%
where the time goes in v2:
time: 244 us; the launch traced here: 242 us
  waiting for transfers between devices  103 us (42%)
  starting transfers between devices  71.8 us (29%)
  Pallas kernels  58.3 us (24%)
  local copies, waits for them, and re-layouts  8.54 us (3%)
    pallas_call x6, Pallas kernels, tile(): pl.pallas_call(functools.partial(tile_body, shifts, relayed), grid_spec=P...  39.7 us
    ppermute x2, waiting for transfers between devices, layer(): piece.append(lax.ppermute(sent, AXES, to))  39.3 us
    ppermute x3, waiting for transfers between devices, layer(): got = lax.ppermute(piece, 'y', ring(shift)) if shift else piece  23.1 us
    ppermute x8, starting transfers between devices, layer(): arrived.append(lax.ppermute(v, AXES, to))  15.9 us
    ppermute x1, waiting for transfers between devices, layer(): oth_1[1] = lax.ppermute(own_0[1], Z, OTHER)  12.3 us
    ppermute x8, waiting for transfers between devices, layer(): arrived.append(lax.ppermute(v, AXES, to))  10.4 us
    ppermute x6, waiting for transfers between devices, layer(): plus = lax.ppermute(plus, 'x', ring(1))  9.14 us
    ppermute x6, starting transfers between devices, layer(): minus = lax.ppermute(minus, 'x', ring(3))  8.92 us
  transfers between devices with their start and end apart: 44, of which 13 were waited for; matrix products, arithmetic and copies ran while one was open for 1% of the time, Pallas kernels for 23%

profile of v2, /device:TPU:1, one launch (start us, length us, event | category | flops | bytes accessed | tf_op | source)
XLA Modules:
  0.0 242.1 jit_solution(17673424336018222583)
XLA Ops:
  1.7 4.7 %collective-permute-start = (bf16[512,1024]{1,0:T(8,128)(2,1)S(1)}, bf16[512,1024]{1,0:T(8,128)(2,1)}, u32[]{:S(2)}, u32[]{:S(2)}) collective-permute-start(bf16[512,1024]{1,0:T(8,128)(2,1)S(1)} %get-tuple-element.84), channel_id=1, source_target_pairs={{4,16},{16,4},{20,0},{0,20},{5,17},{17,5},{21,1},{1,21},{6,18},{18... | collective-permute-start | bytes 3145736 | tf_op jit(solution)/shard_map/ppermute | solution.py:316
  8.4 3.0 %collective-permute-start.6 = (bf16[512,512]{1,0:T(8,128)(2,1)S(1)}, bf16[512,512]{1,0:T(8,128)(2,1)S(1)}, u32[]{:S(2)}, u32[]{:S(2)}) collective-permute-start(bf16[512,512]{1,0:T(8,128)(2,1)S(1)} %get-tuple-element.81), channel_id=1, source_target_pairs={{0,64},{1,96},{2,84},{3,116},{4,68},{5,100},{6,80},{7,112},{8,72},... | collective-permute-start | bytes 1572872 | tf_op jit(solution)/shard_map/ppermute | solution.py:311
  11.3 5.5 %collective-permute-start.4 = (bf16[512,1024]{1,0:T(8,128)(2,1)S(1)}, bf16[512,1024]{1,0:T(8,128)(2,1)S(1)}, u32[]{:S(2)}, u32[]{:S(2)}) collective-permute-start(bf16[512,1024]{1,0:T(8,128)(2,1)S(1)} %get-tuple-element.83), channel_id=1, source_target_pairs={{4,16},{16,4},{20,0},{0,20},{5,17},{17,5},{21,1},{1,21},{6,18},{18... | collective-permute-start | bytes 3145736 | tf_op jit(solution)/shard_map/ppermute | solution.py:318
  17.1 39.3 %collective-permute-done.6.second = bf16[512,512]{1,0:T(8,128)(2,1)S(1)} collective-permute-done((bf16[512,512]{1,0:T(8,128)(2,1)S(1)}, bf16[512,512]{1,0:T(8,128)(2,1)S(1)}, u32[]{:S(2)}, u32[]{:S(2)}) %collective-permute-start.6) | collective-permute-done | bytes 524320 | tf_op jit(solution)/shard_map/ppermute | solution.py:311
  58.1 2.7 %collective-permute-start.31 = (bf16[2,512,512]{2,1,0:T(8,128)(2,1)S(1)}, bf16[2,512,512]{2,1,0:T(8,128)(2,1)}, u32[]{:S(2)}, u32[]{:S(2)}) collective-permute-start(bf16[2,512,512]{2,1,0:T(8,128)(2,1)S(1)} %join.1.refs_4_), channel_id=1, source_target_pairs={{0,96},{32,0},{64,32},{96,64},{1,97},{33,1},{65,33},{97,65},{2,98}... | collective-permute-start | bytes 3145736 | tf_op jit(solution)/shard_map/ppermute | solution.py:325
  60.8 12.3 %collective-permute-done.4 = bf16[512,1024]{1,0:T(8,128)(2,1)S(1)} collective-permute-done((bf16[512,1024]{1,0:T(8,128)(2,1)S(1)}, bf16[512,1024]{1,0:T(8,128)(2,1)S(1)}, u32[]{:S(2)}, u32[]{:S(2)}) %collective-permute-start.4) | collective-permute-done | bytes 1048608 | tf_op jit(solution)/shard_map/ppermute | solution.py:318
  74.1 2.9 %collective-permute-start.18 = (bf16[2,512,512]{2,1,0:T(8,128)(2,1)S(1)}, bf16[2,512,512]{2,1,0:T(8,128)(2,1)}, u32[]{:S(2)}, u32[]{:S(2)}) collective-permute-start(bf16[2,512,512]{2,1,0:T(8,128)(2,1)S(1)} %join.1.refs_4_), channel_id=1, source_target_pairs={{0,64},{32,96},{64,0},{96,32},{1,65},{33,97},{65,1},{97,33},{2,66}... | collective-permute-start | bytes 3145736 | tf_op jit(solution)/shard_map/ppermute | solution.py:325
  79.1 3.4 %collective-permute-start.3 = (bf16[512,1024]{1,0:T(8,128)(2,1)}, bf16[512,1024]{1,0:T(8,128)(2,1)}, u32[]{:S(2)}, u32[]{:S(2)}) collective-permute-start(bf16[512,1024]{1,0:T(8,128)(2,1)} %collective-permute-done.2), channel_id=1, source_target_pairs={{4,16},{16,4},{20,0},{0,20},{5,17},{17,5},{21,1},{1,21},{6,18},{18... | collective-permute-start | bytes 3145736 | tf_op jit(solution)/shard_map/ppermute | solution.py:320
  85.7 21.5 %collective-permute-done.18.refs_4_ = bf16[2,512,512]{2,1,0:T(8,128)(2,1)} collective-permute-done((bf16[2,512,512]{2,1,0:T(8,128)(2,1)S(1)}, bf16[2,512,512]{2,1,0:T(8,128)(2,1)}, u32[]{:S(2)}, u32[]{:S(2)}) %collective-permute-start.18) | collective-permute-done | bytes 1048608 | tf_op jit(solution)/shard_map/ppermute | solution.py:325
  110.3 4.9 %shard_map.39 = (f32[2,128,512]{2,1,0:T(8,128)S(1)}, bf16[2,128,512]{2,1,0:T(8,128)(2,1)S(1)}, bf16[2,128,512]{2,1,0:T(8,128)(2,1)S(1)}, bf16[2,128,512]{2,1,0:T(8,128)(2,1)S(1)}) custom-call(s32[22]{0:T(128)S(1)} %stack.91.scalars, bf16[4,128,1024]{2,1,0:T(8,128)(2,1)S(1)} %bitcast.33, bf16[4,128,1024]{2,1,0:T(8,128)(2,1)S(1)} %bitcast.30, ...), custom_call_target="tpu_custom_call" | custom-call | flops 2147483648 | bytes 1048576 | tf_op jit(solution)/shard_map/pallas_call | solution.py:142
  115.2 4.0 %collective-permute-start.13 = (bf16[2,128,512]{2,1,0:T(8,128)(2,1)S(1)}, bf16[2,128,512]{2,1,0:T(8,128)(2,1)S(1)}, u32[]{:S(2)}, u32[]{:S(2)}) collective-permute-start(bf16[2,128,512]{2,1,0:T(8,128)(2,1)S(1)} %get-tuple-element.50), channel_id=1, source_target_pairs={{0,2},{1,3},{2,0},{3,1},{4,6},{5,7},{6,4},{7,5},{8,10},{9,11},{10,... | collective-permute-start | bytes 786440 | tf_op jit(solution)/shard_map/ppermute | solution.py:333
  119.2 5.3 %collective-permute-start.14 = (bf16[2,128,512]{2,1,0:T(8,128)(2,1)S(1)}, bf16[2,128,512]{2,1,0:T(8,128)(2,1)S(1)}, u32[]{:S(2)}, u32[]{:S(2)}) collective-permute-start(bf16[2,128,512]{2,1,0:T(8,128)(2,1)S(1)} %get-tuple-element.51), channel_id=1, source_target_pairs={{0,1},{1,2},{2,3},{3,0},{4,5},{5,6},{6,7},{7,4},{8,9},{9,10},{10,1... | collective-permute-start | bytes 786440 | tf_op jit(solution)/shard_map/ppermute | solution.py:331
  124.5 5.4 %shard_map.37 = (f32[2,128,512]{2,1,0:T(8,128)S(1)}, f32[2,128,512]{2,1,0:T(8,128)S(1)}, bf16[2,128,512]{2,1,0:T(8,128)(2,1)S(1)}, bf16[2,128,512]{2,1,0:T(8,128)(2,1)S(1)}) custom-call(s32[22]{0:T(128)S(1)} %stack.91.scalars, bf16[4,128,1024]{2,1,0:T(8,128)(2,1)} %bitcast.22.refs_0_, bf16[4,128,1024]{2,1,0:T(8,128)(2,1)} %bitcast.23.refs_1_, ...), custom_call_target="tpu_custom_call" | custom-call | flops 2147483648 | bytes 1048576 | tf_op jit(solution)/shard_map/pallas_call | solution.py:142
  131.5 9.5 %shard_map.47 = (f32[2,128,1024]{2,1,0:T(8,128)S(1)}, f32[2,128,1024]{2,1,0:T(8,128)S(1)}, bf16[2,128,1024]{2,1,0:T(8,128)(2,1)S(1)}, bf16[2,128,1024]{2,1,0:T(8,128)(2,1)S(1)}) custom-call(s32[22]{0:T(128)S(1)} %stack.91.scalars, bf16[4,128,1024]{2,1,0:T(8,128)(2,1)} %bitcast.22.refs_0_, bf16[4,128,1024]{2,1,0:T(8,128)(2,1)} %bitcast.23.refs_1_, ...), custom_call_target="tpu_custom_call" | custom-call | flops 4294967296 | bytes 1048576 | tf_op jit(solution)/shard_map/pallas_call | solution.py:142
  142.7 2.5 %collective-permute-start.34 = (bf16[2,128,1024]{2,1,0:T(8,128)(2,1)S(1)}, bf16[2,128,1024]{2,1,0:T(8,128)(2,1)S(1)}, u32[]{:S(2)}, u32[]{:S(2)}) collective-permute-start(bf16[2,128,1024]{2,1,0:T(8,128)(2,1)S(1)} %get-tuple-element.69), channel_id=1, source_target_pairs={{0,3},{1,0},{2,1},{3,2},{4,7},{5,4},{6,5},{7,6},{8,11},{9,8},{10,9... | collective-permute-start | bytes 1572872 | tf_op jit(solution)/shard_map/ppermute | solution.py:342
  145.2 9.0 %shard_map.49 = (f32[2,128,1024]{2,1,0:T(8,128)S(1)}, bf16[2,128,1024]{2,1,0:T(8,128)(2,1)S(1)}, bf16[2,128,1024]{2,1,0:T(8,128)(2,1)S(1)}, bf16[2,128,1024]{2,1,0:T(8,128)(2,1)S(1)}) custom-call(s32[22]{0:T(128)S(1)} %stack.91.scalars, bf16[4,128,1024]{2,1,0:T(8,128)(2,1)S(1)} %bitcast.34, bf16[4,128,1024]{2,1,0:T(8,128)(2,1)S(1)} %bitcast.31, ...), custom_call_target="tpu_custom_call" | custom-call | flops 4294967296 | bytes 1048576 | tf_op jit(solution)/shard_map/pallas_call | solution.py:142
  154.3 5.8 %shard_map.42 = (f32[2,128,512]{2,1,0:T(8,128)S(1)}, f32[2,128,512]{2,1,0:T(8,128)S(1)}, bf16[2,128,512]{2,1,0:T(8,128)(2,1)S(1)}, bf16[2,128,512]{2,1,0:T(8,128)(2,1)S(1)}) custom-call(s32[22]{0:T(128)S(1)} %stack.91.scalars, bf16[4,128,1024]{2,1,0:T(8,128)(2,1)} %bitcast.22.refs_0_, bf16[4,128,1024]{2,1,0:T(8,128)(2,1)} %bitcast.23.refs_1_, ...), custom_call_target="tpu_custom_call" | custom-call | flops 2147483648 | bytes 1048576 | tf_op jit(solution)/shard_map/pallas_call | solution.py:142
  160.7 2.1 collective-permute-start.21
  162.8 2.7 %collective-permute-start.39 = (bf16[2,128,1024]{2,1,0:T(8,128)(2,1)S(1)}, bf16[2,128,1024]{2,1,0:T(8,128)(2,1)S(1)}, u32[]{:S(2)}, u32[]{:S(2)}) collective-permute-start(bf16[2,128,1024]{2,1,0:T(8,128)(2,1)S(1)} %get-tuple-element.76), channel_id=1, source_target_pairs={{0,3},{1,0},{2,1},{3,2},{4,7},{5,4},{6,5},{7,6},{8,11},{9,8},{10,9... | collective-permute-start | bytes 1572872 | tf_op jit(solution)/shard_map/ppermute | solution.py:332
  166.8 8.5 %collective-permute-done.20.plus.refs_1_ = bf16[2,128,512]{2,1,0:T(8,128)(2,1)S(1)} collective-permute-done((bf16[2,128,512]{2,1,0:T(8,128)(2,1)S(1)}, bf16[2,128,512]{2,1,0:T(8,128)(2,1)S(1)}, u32[]{:S(2)}, u32[]{:S(2)}) %collective-permute-start.20) | collective-permute-done | bytes 262176 | tf_op jit(solution)/shard_map/ppermute | solution.py:341
  176.7 3.4 %collective-permute-start.36 = (bf16[2,128,512]{2,1,0:T(8,128)(2,1)S(1)}, bf16[2,128,512]{2,1,0:T(8,128)(2,1)S(1)}, u32[]{:S(2)}, u32[]{:S(2)}) collective-permute-start(bf16[2,128,512]{2,1,0:T(8,128)(2,1)S(1)} %get-tuple-element.72), channel_id=1, source_target_pairs={{0,3},{1,0},{2,1},{3,2},{4,7},{5,4},{6,5},{7,6},{8,11},{9,8},{10,9... | collective-permute-start | bytes 786440 | tf_op jit(solution)/shard_map/ppermute | solution.py:345
  180.1 5.2 %shard_map.44 = (f32[2,128,512]{2,1,0:T(8,128)S(1)}, bf16[2,128,512]{2,1,0:T(8,128)(2,1)S(1)}, bf16[2,128,512]{2,1,0:T(8,128)(2,1)S(1)}, bf16[2,128,512]{2,1,0:T(8,128)(2,1)S(1)}) custom-call(s32[22]{0:T(128)S(1)} %stack.91.scalars, bf16[4,128,1024]{2,1,0:T(8,128)(2,1)S(1)} %bitcast.35, bf16[4,128,1024]{2,1,0:T(8,128)(2,1)S(1)} %bitcast.32, ...), custom_call_target="tpu_custom_call" | custom-call | flops 2147483648 | bytes 1048576 | tf_op jit(solution)/shard_map/pallas_call | solution.py:142
  189.2 4.9 %collective-permute-done.35.refs_3_ = bf16[2,128,512]{2,1,0:T(8,128)(2,1)S(1)} collective-permute-done((bf16[2,128,512]{2,1,0:T(8,128)(2,1)S(1)}, bf16[2,128,512]{2,1,0:T(8,128)(2,1)S(1)}, u32[]{:S(2)}, u32[]{:S(2)}) %collective-permute-start.35) | collective-permute-done | bytes 262176 | tf_op jit(solution)/shard_map/ppermute | solution.py:344
  197.4 2.1 shard_map.51
  200.8 6.7 %collective-permute-start.40 = (bf16[2,128,512]{2,1,0:T(8,128)(2,1)S(1)}, bf16[2,128,512]{2,1,0:T(8,128)(2,1)S(1)}, u32[]{:S(2)}, u32[]{:S(2)}) collective-permute-start(bf16[2,128,512]{2,1,0:T(8,128)(2,1)S(1)} %get-tuple-element.77), channel_id=1, source_target_pairs={{0,96},{1,97},{2,98},{3,99},{4,104},{5,105},{6,106},{7,107},{8,100... | collective-permute-start | bytes 786440 | tf_op jit(solution)/shard_map/ppermute | solution.py:353
  212.3 2.0 collective-permute-start.43
  215.7 2.2 collective-permute-start.27
  223.1 3.1 %collective-permute-done.43.refs_3_ = bf16[2,128,512]{2,1,0:T(8,128)(2,1)S(1)} collective-permute-done((bf16[2,128,512]{2,1,0:T(8,128)(2,1)S(1)}, bf16[2,128,512]{2,1,0:T(8,128)(2,1)S(1)}, u32[]{:S(2)}, u32[]{:S(2)}) %collective-permute-start.43) | collective-permute-done | bytes 262176 | tf_op jit(solution)/shard_map/ppermute | solution.py:353
  226.2 3.9 %shard_map.52.refs_3_ = bf16[16,128,512]{2,1,0:T(8,128)(2,1)} custom-call(s32[22]{0:T(128)S(1)} %stack.91.scalars, bf16[2,128,512]{2,1,0:T(8,128)(2,1)S(1)} %collective-permute-done.40.refs_0_, bf16[2,128,512]{2,1,0:T(8,128)(2,1)S(1)} %collective-permute-done.41.refs_1_, bf16[2,128,512]{2,1,0:T(8,128)(2,1)S(1)} %collective-permute-done.42.refs_2_, ...), custom_call_target="tpu_custom_call" | custom-call | flops 1073741824 | bytes 4194304 | tf_op jit(solution)/shard_map/pallas_call | solution.py:272
  230.5 6.9 %collective-permute-done.28.refs_1_ = bf16[2,128,512]{2,1,0:T(8,128)(2,1)S(1)} collective-permute-done((bf16[2,128,512]{2,1,0:T(8,128)(2,1)S(1)}, bf16[2,128,512]{2,1,0:T(8,128)(2,1)S(1)}, u32[]{:S(2)}, u32[]{:S(2)}) %collective-permute-start.28) | collective-permute-done | bytes 262176 | tf_op jit(solution)/shard_map/ppermute | solution.py:353
  237.4 2.3 shard_map.53.refs_3_
  239.7 2.3 shard_map.54
  (96 shorter events, 41.8 us)
Async XLA Ops:
  1.7 56.4 %collective-permute-start = (bf16[512,1024]{1,0:T(8,128)(2,1)S(1)}, bf16[512,1024]{1,0:T(8,128)(2,1)}, u32[]{:S(2)}, u32[]{:S(2)}) collective-permute-start(bf16[512,1024]{1,0:T(8,128)(2,1)S(1)} %get-tuple-element.84), channel_id=1, source_target_pairs={{4,16},{16,4},{20,0},{0,20},{5,17},{17,5},{21,1},{1,21},{6,18},{18... | collective-permute-start | bytes 3145736 | tf_op jit(solution)/shard_map/ppermute | solution.py:316
  6.4 51.8 %collective-permute-start.2 = (bf16[512,1024]{1,0:T(8,128)(2,1)S(1)}, bf16[512,1024]{1,0:T(8,128)(2,1)}, u32[]{:S(2)}, u32[]{:S(2)}) collective-permute-start(bf16[512,1024]{1,0:T(8,128)(2,1)S(1)} %get-tuple-element.83), channel_id=1, source_target_pairs={{0,4},{4,0},{16,20},{20,16},{1,5},{5,1},{17,21},{21,17},{2,6},{6,2... | collective-permute-start | bytes 3145736 | tf_op jit(solution)/shard_map/ppermute | solution.py:315
  8.4 48.0 %collective-permute-start.6 = (bf16[512,512]{1,0:T(8,128)(2,1)S(1)}, bf16[512,512]{1,0:T(8,128)(2,1)S(1)}, u32[]{:S(2)}, u32[]{:S(2)}) collective-permute-start(bf16[512,512]{1,0:T(8,128)(2,1)S(1)} %get-tuple-element.81), channel_id=1, source_target_pairs={{0,64},{1,96},{2,84},{3,116},{4,68},{5,100},{6,80},{7,112},{8,72},... | collective-permute-start | bytes 1572872 | tf_op jit(solution)/shard_map/ppermute | solution.py:311
  11.3 61.8 %collective-permute-start.4 = (bf16[512,1024]{1,0:T(8,128)(2,1)S(1)}, bf16[512,1024]{1,0:T(8,128)(2,1)S(1)}, u32[]{:S(2)}, u32[]{:S(2)}) collective-permute-start(bf16[512,1024]{1,0:T(8,128)(2,1)S(1)} %get-tuple-element.83), channel_id=1, source_target_pairs={{4,16},{16,4},{20,0},{0,20},{5,17},{17,5},{21,1},{1,21},{6,18},{18... | collective-permute-start | bytes 3145736 | tf_op jit(solution)/shard_map/ppermute | solution.py:318
  16.8 60.2 %collective-permute-start.12 = (bf16[512,1024]{1,0:T(8,128)(2,1)S(1)}, bf16[512,1024]{1,0:T(8,128)(2,1)S(1)}, u32[]{:S(2)}, u32[]{:S(2)}) collective-permute-start(bf16[512,1024]{1,0:T(8,128)(2,1)S(1)} %get-tuple-element.84), channel_id=1, source_target_pairs={{0,4},{4,0},{16,20},{20,16},{1,5},{5,1},{17,21},{21,17},{2,6},{6,2... | collective-permute-start | bytes 3145736 | tf_op jit(solution)/shard_map/ppermute | solution.py:317
  56.5 21.6 %collective-permute-start.7 = (bf16[2,512,512]{2,1,0:T(8,128)(2,1)S(1)}, bf16[2,512,512]{2,1,0:T(8,128)(2,1)S(1)}, u32[]{:S(2)}, u32[]{:S(2)}) collective-permute-start(bf16[2,512,512]{2,1,0:T(8,128)(2,1)S(1)} %join.1.refs_4_), channel_id=1, source_target_pairs={{0,8},{8,0},{1,9},{9,1},{2,10},{10,2},{3,11},{11,3},{4,12},{12,4},... | collective-permute-start | bytes 3145736 | tf_op jit(solution)/shard_map/ppermute | solution.py:326
  58.1 25.9 %collective-permute-start.29 = (bf16[2,512,512]{2,1,0:T(8,128)(2,1)S(1)}, bf16[2,512,512]{2,1,0:T(8,128)(2,1)}, u32[]{:S(2)}, u32[]{:S(2)}) collective-permute-start(bf16[2,512,512]{2,1,0:T(8,128)(2,1)S(1)} %join.1.refs_4_), channel_id=1, source_target_pairs={{0,32},{32,64},{64,96},{96,0},{1,33},{33,65},{65,97},{97,1},{2,34}... | collective-permute-start | bytes 3145736 | tf_op jit(solution)/shard_map/ppermute | solution.py:325
  58.1 26.9 %collective-permute-start.31 = (bf16[2,512,512]{2,1,0:T(8,128)(2,1)S(1)}, bf16[2,512,512]{2,1,0:T(8,128)(2,1)}, u32[]{:S(2)}, u32[]{:S(2)}) collective-permute-start(bf16[2,512,512]{2,1,0:T(8,128)(2,1)S(1)} %join.1.refs_4_), channel_id=1, source_target_pairs={{0,96},{32,0},{64,32},{96,64},{1,97},{33,1},{65,33},{97,65},{2,98}... | collective-permute-start | bytes 3145736 | tf_op jit(solution)/shard_map/ppermute | solution.py:325
  74.1 33.0 %collective-permute-start.18 = (bf16[2,512,512]{2,1,0:T(8,128)(2,1)S(1)}, bf16[2,512,512]{2,1,0:T(8,128)(2,1)}, u32[]{:S(2)}, u32[]{:S(2)}) collective-permute-start(bf16[2,512,512]{2,1,0:T(8,128)(2,1)S(1)} %join.1.refs_4_), channel_id=1, source_target_pairs={{0,64},{32,96},{64,0},{96,32},{1,65},{33,97},{65,1},{97,33},{2,66}... | collective-permute-start | bytes 3145736 | tf_op jit(solution)/shard_map/ppermute | solution.py:325
  78.1 37.1 %collective-permute-start.1 = (bf16[512,1024]{1,0:T(8,128)(2,1)}, bf16[512,1024]{1,0:T(8,128)(2,1)}, u32[]{:S(2)}, u32[]{:S(2)}) collective-permute-start(bf16[512,1024]{1,0:T(8,128)(2,1)} %collective-permute-done), channel_id=1, source_target_pairs={{0,4},{4,0},{16,20},{20,16},{1,5},{5,1},{17,21},{21,17},{2,6},{6,2... | collective-permute-start | bytes 3145736 | tf_op jit(solution)/shard_map/ppermute | solution.py:319
  79.1 40.1 %collective-permute-start.3 = (bf16[512,1024]{1,0:T(8,128)(2,1)}, bf16[512,1024]{1,0:T(8,128)(2,1)}, u32[]{:S(2)}, u32[]{:S(2)}) collective-permute-start(bf16[512,1024]{1,0:T(8,128)(2,1)} %collective-permute-done.2), channel_id=1, source_target_pairs={{4,16},{16,4},{20,0},{0,20},{5,17},{17,5},{21,1},{1,21},{6,18},{18... | collective-permute-start | bytes 3145736 | tf_op jit(solution)/shard_map/ppermute | solution.py:320
  84.1 45.8 %collective-permute-start.30 = (bf16[2,512,512]{2,1,0:T(8,128)(2,1)}, bf16[2,512,512]{2,1,0:T(8,128)(2,1)}, u32[]{:S(2)}, u32[]{:S(2)}) collective-permute-start(bf16[2,512,512]{2,1,0:T(8,128)(2,1)} %collective-permute-done.29.refs_4_), channel_id=1, source_target_pairs={{0,8},{8,0},{1,9},{9,1},{2,10},{10,2},{3,11},{11,3},{4,12},{12,4},... | collective-permute-start | bytes 3145736 | tf_op jit(solution)/shard_map/ppermute | solution.py:326
  85.0 45.0 %collective-permute-start.32 = (bf16[2,512,512]{2,1,0:T(8,128)(2,1)}, bf16[2,512,512]{2,1,0:T(8,128)(2,1)}, u32[]{:S(2)}, u32[]{:S(2)}) collective-permute-start(bf16[2,512,512]{2,1,0:T(8,128)(2,1)} %collective-permute-done.31.refs_6_), channel_id=1, source_target_pairs={{0,8},{8,0},{1,9},{9,1},{2,10},{10,2},{3,11},{11,3},{4,12},{12,4},... | collective-permute-start | bytes 3145736 | tf_op jit(solution)/shard_map/ppermute | solution.py:326
  107.2 47.0 %collective-permute-start.19 = (bf16[2,512,512]{2,1,0:T(8,128)(2,1)}, bf16[2,512,512]{2,1,0:T(8,128)(2,1)S(1)}, u32[]{:S(2)}, u32[]{:S(2)}) collective-permute-start(bf16[2,512,512]{2,1,0:T(8,128)(2,1)} %collective-permute-done.18.refs_4_), channel_id=1, source_target_pairs={{0,8},{8,0},{1,9},{9,1},{2,10},{10,2},{3,11},{11,3},{4,12},{12,4},... | collective-permute-start | bytes 3145736 | tf_op jit(solution)/shard_map/ppermute | solution.py:326
  115.2 25.7 %collective-permute-start.13 = (bf16[2,128,512]{2,1,0:T(8,128)(2,1)S(1)}, bf16[2,128,512]{2,1,0:T(8,128)(2,1)S(1)}, u32[]{:S(2)}, u32[]{:S(2)}) collective-permute-start(bf16[2,128,512]{2,1,0:T(8,128)(2,1)S(1)} %get-tuple-element.50), channel_id=1, source_target_pairs={{0,2},{1,3},{2,0},{3,1},{4,6},{5,7},{6,4},{7,5},{8,10},{9,11},{10,... | collective-permute-start | bytes 786440 | tf_op jit(solution)/shard_map/ppermute | solution.py:333
  119.2 23.3 %collective-permute-start.14 = (bf16[2,128,512]{2,1,0:T(8,128)(2,1)S(1)}, bf16[2,128,512]{2,1,0:T(8,128)(2,1)S(1)}, u32[]{:S(2)}, u32[]{:S(2)}) collective-permute-start(bf16[2,128,512]{2,1,0:T(8,128)(2,1)S(1)} %get-tuple-element.51), channel_id=1, source_target_pairs={{0,1},{1,2},{2,3},{3,0},{4,5},{5,6},{6,7},{7,4},{8,9},{9,10},{10,1... | collective-permute-start | bytes 786440 | tf_op jit(solution)/shard_map/ppermute | solution.py:331
  130.0 30.0 %collective-permute-start.8 = (bf16[2,128,512]{2,1,0:T(8,128)(2,1)S(1)}, bf16[2,128,512]{2,1,0:T(8,128)(2,1)S(1)}, u32[]{:S(2)}, u32[]{:S(2)}) collective-permute-start(bf16[2,128,512]{2,1,0:T(8,128)(2,1)S(1)} %get-tuple-element.44), channel_id=1, source_target_pairs={{0,1},{1,2},{2,3},{3,0},{4,5},{5,6},{6,7},{7,4},{8,9},{9,10},{10,1... | collective-permute-start | bytes 786440 | tf_op jit(solution)/shard_map/ppermute | solution.py:341
  141.0 19.7 %collective-permute-start.9 = (bf16[2,128,512]{2,1,0:T(8,128)(2,1)S(1)}, bf16[2,128,512]{2,1,0:T(8,128)(2,1)S(1)}, u32[]{:S(2)}, u32[]{:S(2)}) collective-permute-start(bf16[2,128,512]{2,1,0:T(8,128)(2,1)S(1)} %get-tuple-element.45), channel_id=1, source_target_pairs={{0,3},{1,0},{2,1},{3,2},{4,7},{5,4},{6,5},{7,6},{8,11},{9,8},{10,9... | collective-permute-start | bytes 786440 | tf_op jit(solution)/shard_map/ppermute | solution.py:342
  142.5 20.3 %collective-permute-start.33 = (bf16[2,128,1024]{2,1,0:T(8,128)(2,1)S(1)}, bf16[2,128,1024]{2,1,0:T(8,128)(2,1)S(1)}, u32[]{:S(2)}, u32[]{:S(2)}) collective-permute-start(bf16[2,128,1024]{2,1,0:T(8,128)(2,1)S(1)} %get-tuple-element.68), channel_id=1, source_target_pairs={{0,1},{1,2},{2,3},{3,0},{4,5},{5,6},{6,7},{7,4},{8,9},{9,10},{10,1... | collective-permute-start | bytes 1572872 | tf_op jit(solution)/shard_map/ppermute | solution.py:341
  142.7 20.2 %collective-permute-start.34 = (bf16[2,128,1024]{2,1,0:T(8,128)(2,1)S(1)}, bf16[2,128,1024]{2,1,0:T(8,128)(2,1)S(1)}, u32[]{:S(2)}, u32[]{:S(2)}) collective-permute-start(bf16[2,128,1024]{2,1,0:T(8,128)(2,1)S(1)} %get-tuple-element.69), channel_id=1, source_target_pairs={{0,3},{1,0},{2,1},{3,2},{4,7},{5,4},{6,5},{7,6},{8,11},{9,8},{10,9... | collective-permute-start | bytes 1572872 | tf_op jit(solution)/shard_map/ppermute | solution.py:342
  154.2 31.1 %collective-permute-start.37 = (bf16[2,128,1024]{2,1,0:T(8,128)(2,1)S(1)}, bf16[2,128,1024]{2,1,0:T(8,128)(2,1)S(1)}, u32[]{:S(2)}, u32[]{:S(2)}) collective-permute-start(bf16[2,128,1024]{2,1,0:T(8,128)(2,1)S(1)} %get-tuple-element.74), channel_id=1, source_target_pairs={{0,2},{1,3},{2,0},{3,1},{4,6},{5,7},{6,4},{7,5},{8,10},{9,11},{10,... | collective-permute-start | bytes 1572872 | tf_op jit(solution)/shard_map/ppermute | solution.py:333
  160.7 16.0 %collective-permute-start.21 = (bf16[2,128,512]{2,1,0:T(8,128)(2,1)S(1)}, bf16[2,128,512]{2,1,0:T(8,128)(2,1)S(1)}, u32[]{:S(2)}, u32[]{:S(2)}) collective-permute-start(bf16[2,128,512]{2,1,0:T(8,128)(2,1)S(1)} %get-tuple-element.57), channel_id=1, source_target_pairs={{0,3},{1,0},{2,1},{3,2},{4,7},{5,4},{6,5},{7,6},{8,11},{9,8},{10,9... | collective-permute-start | bytes 786440 | tf_op jit(solution)/shard_map/ppermute | solution.py:342
  162.8 23.7 %collective-permute-start.38 = (bf16[2,128,1024]{2,1,0:T(8,128)(2,1)S(1)}, bf16[2,128,1024]{2,1,0:T(8,128)(2,1)S(1)}, u32[]{:S(2)}, u32[]{:S(2)}) collective-permute-start(bf16[2,128,1024]{2,1,0:T(8,128)(2,1)S(1)} %get-tuple-element.75), channel_id=1, source_target_pairs={{0,1},{1,2},{2,3},{3,0},{4,5},{5,6},{6,7},{7,4},{8,9},{9,10},{10,1... | collective-permute-start | bytes 1572872 | tf_op jit(solution)/shard_map/ppermute | solution.py:331
  162.8 25.1 %collective-permute-start.39 = (bf16[2,128,1024]{2,1,0:T(8,128)(2,1)S(1)}, bf16[2,128,1024]{2,1,0:T(8,128)(2,1)S(1)}, u32[]{:S(2)}, u32[]{:S(2)}) collective-permute-start(bf16[2,128,1024]{2,1,0:T(8,128)(2,1)S(1)} %get-tuple-element.76), channel_id=1, source_target_pairs={{0,3},{1,0},{2,1},{3,2},{4,7},{5,4},{6,5},{7,6},{8,11},{9,8},{10,9... | collective-permute-start | bytes 1572872 | tf_op jit(solution)/shard_map/ppermute | solution.py:332
  175.2 18.9 %collective-permute-start.35 = (bf16[2,128,512]{2,1,0:T(8,128)(2,1)S(1)}, bf16[2,128,512]{2,1,0:T(8,128)(2,1)S(1)}, u32[]{:S(2)}, u32[]{:S(2)}) collective-permute-start(bf16[2,128,512]{2,1,0:T(8,128)(2,1)S(1)} %get-tuple-element.71), channel_id=1, source_target_pairs={{0,1},{1,2},{2,3},{3,0},{4,5},{5,6},{6,7},{7,4},{8,9},{9,10},{10,1... | collective-permute-start | bytes 786440 | tf_op jit(solution)/shard_map/ppermute | solution.py:344
  176.7 19.1 %collective-permute-start.36 = (bf16[2,128,512]{2,1,0:T(8,128)(2,1)S(1)}, bf16[2,128,512]{2,1,0:T(8,128)(2,1)S(1)}, u32[]{:S(2)}, u32[]{:S(2)}) collective-permute-start(bf16[2,128,512]{2,1,0:T(8,128)(2,1)S(1)} %get-tuple-element.72), channel_id=1, source_target_pairs={{0,3},{1,0},{2,1},{3,2},{4,7},{5,4},{6,5},{7,6},{8,11},{9,8},{10,9... | collective-permute-start | bytes 786440 | tf_op jit(solution)/shard_map/ppermute | solution.py:345
  187.9 20.4 %collective-permute-start.25 = (bf16[2,128,512]{2,1,0:T(8,128)(2,1)S(1)}, bf16[2,128,512]{2,1,0:T(8,128)(2,1)S(1)}, u32[]{:S(2)}, u32[]{:S(2)}) collective-permute-start(bf16[2,128,512]{2,1,0:T(8,128)(2,1)S(1)} %get-tuple-element.63), channel_id=1, source_target_pairs={{0,1},{1,2},{2,3},{3,0},{4,5},{5,6},{6,7},{7,4},{8,9},{9,10},{10,1... | collective-permute-start | bytes 786440 | tf_op jit(solution)/shard_map/ppermute | solution.py:331
  194.1 16.1 %collective-permute-start.26 = (bf16[2,128,512]{2,1,0:T(8,128)(2,1)S(1)}, bf16[2,128,512]{2,1,0:T(8,128)(2,1)S(1)}, u32[]{:S(2)}, u32[]{:S(2)}) collective-permute-start(bf16[2,128,512]{2,1,0:T(8,128)(2,1)S(1)} %get-tuple-element.64), channel_id=1, source_target_pairs={{0,3},{1,0},{2,1},{3,2},{4,7},{5,4},{6,5},{7,6},{8,11},{9,8},{10,9... | collective-permute-start | bytes 786440 | tf_op jit(solution)/shard_map/ppermute | solution.py:332
  200.8 17.1 %collective-permute-start.40 = (bf16[2,128,512]{2,1,0:T(8,128)(2,1)S(1)}, bf16[2,128,512]{2,1,0:T(8,128)(2,1)S(1)}, u32[]{:S(2)}, u32[]{:S(2)}) collective-permute-start(bf16[2,128,512]{2,1,0:T(8,128)(2,1)S(1)} %get-tuple-element.77), channel_id=1, source_target_pairs={{0,96},{1,97},{2,98},{3,99},{4,104},{5,105},{6,106},{7,107},{8,100... | collective-permute-start | bytes 786440 | tf_op jit(solution)/shard_map/ppermute | solution.py:353
  217.9 19.5 %collective-permute-start.28 = (bf16[2,128,512]{2,1,0:T(8,128)(2,1)S(1)}, bf16[2,128,512]{2,1,0:T(8,128)(2,1)S(1)}, u32[]{:S(2)}, u32[]{:S(2)}) collective-permute-start(bf16[2,128,512]{2,1,0:T(8,128)(2,1)S(1)} %get-tuple-element.66), channel_id=1, source_target_pairs={{0,68},{1,69},{2,70},{3,71},{4,76},{5,77},{6,78},{7,79},{8,64},{9,... | collective-permute-start | bytes 786440 | tf_op jit(solution)/shard_map/ppermute | solution.py:353
  221.1 18.7 %collective-permute-start.16 = (bf16[2,128,512]{2,1,0:T(8,128)(2,1)S(1)}, bf16[2,128,512]{2,1,0:T(8,128)(2,1)S(1)}, u32[]{:S(2)}, u32[]{:S(2)}) collective-permute-start(bf16[2,128,512]{2,1,0:T(8,128)(2,1)S(1)} %get-tuple-element.53), channel_id=1, source_target_pairs={{0,0},{1,1},{2,2},{3,3},{4,8},{5,9},{6,10},{7,11},{8,4},{9,5},{10,... | collective-permute-start | bytes 786440 | tf_op jit(solution)/shard_map/ppermute | solution.py:353
  223.0 16.7 %collective-permute-start.17 = (bf16[2,128,512]{2,1,0:T(8,128)(2,1)S(1)}, bf16[2,128,512]{2,1,0:T(8,128)(2,1)S(1)}, u32[]{:S(2)}, u32[]{:S(2)}) collective-permute-start(bf16[2,128,512]{2,1,0:T(8,128)(2,1)S(1)} %get-tuple-element.54), channel_id=1, source_target_pairs={{0,4},{1,5},{2,6},{3,7},{4,12},{5,13},{6,14},{7,15},{8,0},{9,1},{1... | collective-permute-start | bytes 786440 | tf_op jit(solution)/shard_map/ppermute | solution.py:353
  (21 other events, 212.0 us)
